TPU v7x, 32 devices: a whole 2x2x4 slice. The times are simulated.
32 devices in a mesh: dp: 4 (over x, core), mp: 8 (over z, y).
Axes of the slice: x: 2, y: 2, z: 4, core: 2. Of those that a mesh axis runs over, the one named last changes fastest.
Arguments:
- packed_token_rows: int32 [16, 1024], P('dp'), may hold values from 0 to 44799
- example_numbers: int32 [16, 1024], P('dp'), may hold values from 0 to 15, never falling along the last dimension, each value on 1 to 128 neighbouring positions
- completion: int32 [16, 1024], P('dp'), may hold values 0 or 1
- global_token_count: int32 [], replicated, may hold values from 4096 to 8191
- owners: int32 [4, 4], replicated, may hold values from 0 to 3
- optimizer_step: int32 [], replicated, may hold values from 1 to 20
- embedding: bfloat16 [51200, 1024], P('mp'), may hold values from -0.375 to 0.375
- positions: bfloat16 [1024, 1024], replicated, may hold values from -0.3984375 to 0.3984375
- gains: float32 [3, 1024], replicated, may hold values from 0.1 to 1.9
- query_key_value_weight: bfloat16 [1024, 3, 1024], P(None, None, 'mp'), may hold values from -0.1875 to 0.1875
- attention_output_weight: bfloat16 [1024, 1024], P('mp'), may hold values from -0.75 to 0.75
- feedforward_input_weight: bfloat16 [1024, 4096], P(None, 'mp'), may hold values from -0.1875 to 0.1875
- feedforward_output_weight: bfloat16 [1024, 4096], P(None, 'mp'), may hold values from -0.09375 to 0.09375
- adapter_down_weight: bfloat16 [2, 4, 1024], replicated, may hold values from -0.1875 to 0.1875
- adapter_up_weight: bfloat16 [2, 4, 1024], P(None, None, 'mp'), may hold values from -0.19921875 to 0.19921875
- master: float32 [4, 4, 1024], P(None, None, 'mp'), may hold values from -0.2 to 0.2
- first_moment: float32 [4, 4, 1024], P(None, None, 'mp'), may hold values from -0.006 to 0.006
- second_moment: float32 [4, 4, 1024], P(None, None, 'mp'), may hold values from 1e-08 to 1e-07
Outputs:
- completion_loss: float32 [], replicated
- grad_norm: float32 [], replicated
- new_first: float32 [4, 4, 4, 1024], P('dp', None, None, 'mp')
- new_second: float32 [4, 4, 4, 1024], P('dp', None, None, 'mp')
- new_master: float32 [4, 4, 4, 1024], P('dp', None, None, 'mp')
- new_copy: bfloat16 [4, 4, 4, 1024], P('dp', None, None, 'mp')
Inputs may be any that keep to these rules, and one draw needn't show every extreme that they name: `example_numbers`: never falling along a row.
All inputs are finite; a program needn't handle non-finite values. No bound on the sum of `completion` on one device may be relied on, other than what follows from the above.
Results may differ from a plain program's by a relative error of at most 0.015.
Values may be sent and summed in bfloat16 or wider, within the bound.
A program may use at most 192 MiB of HBM per device.

v0:
```python
import jax
import jax.numpy as jnp
from jax import lax
from jax.sharding import PartitionSpec as P

HEAD_DIM = 64
MICRO = 4


EPS_NORM = 1e-05
ADAPTER_SCALE = 8.0
SCORE_SCALE = 0.125
MASK_VALUE = -1e30
CLIP_NORM = 1.0
BETA_ONE = 0.9
BETA_TWO = 0.999
LEARN_RATE = 0.01
WEIGHT_DECAY = 0.01
ADAM_EPS = 1e-08
CONTRACT_FINAL = (((1,), (1,)), ((), ()))
CONTRACT_FIRST = (((0,), (0,)), ((), ()))


def joined(shard, axis, combine):
    everything = jax.tree.map(lambda part: lax.all_gather(part, axis), shard)
    first = jax.tree.map(lambda part: part[0], everything)

    def lap(k, so_far):
        return combine(so_far, jax.tree.map(lambda part: part[k], everything))

    return lax.fori_loop(1, lax.axis_size(axis), lap, first)


def layer_norm(values, gain_row):
    center = values - jnp.mean(values, axis=-1, keepdims=True)
    spread = jnp.mean(center * center, axis=-1, keepdims=True)
    return center * lax.rsqrt(spread + EPS_NORM) * gain_row


def norm_back(values, gain_row, grad_out):
    return jax.vjp(lambda inner_val: layer_norm(inner_val, gain_row), values)[1](grad_out)[0]


def gelu_back(fc_inner, grad_out):
    return jax.vjp(lambda gelu_in: jax.nn.gelu(gelu_in, approximate=True), fc_inner)[1](grad_out)[0]


def rows_of(array_in, first_row, row_count):
    return lax.dynamic_slice_in_dim(array_in, first_row, row_count, 0)


def by_blocks(row_fn, row_count, block_rows):
    starts = block_rows * jnp.arange(row_count // block_rows, dtype=jnp.int32)
    pieces = lax.map(lambda block_first: row_fn(block_first, block_rows), starts)
    return pieces.reshape((row_count,) + pieces.shape[2:])


def combine_stats(first_set, second_set):
    row_peak = jnp.maximum(first_set[0], second_set[0])
    row_total = first_set[1] * jnp.exp(first_set[0] - row_peak) + second_set[1] * jnp.exp(
        second_set[0] - row_peak
    )
    return (row_peak, row_total, first_set[2] + second_set[2])


def allowed_mask(seg_row, first_row, row_count):
    rows_index = first_row + jnp.arange(row_count, dtype=jnp.int32)
    cols_index = jnp.arange(seg_row.shape[0], dtype=jnp.int32)
    seg_rows = lax.dynamic_slice_in_dim(seg_row, first_row, row_count, 0)
    return (cols_index[None, :] <= rows_index[:, None]) & (seg_row[None, :] == seg_rows[:, None])


def masked_scores(query_blk, key_seq, allowed):
    scores = (
        jnp.einsum("qhd,khd->hqk", query_blk, key_seq, preferred_element_type=jnp.float32)
        * SCORE_SCALE
    )
    return jnp.where(allowed[None], scores, MASK_VALUE)


def attend_all(query_matrix, keys_all, value_matrix_whole, seg_blk, block_rows):
    mixed_parts = []
    log_parts = []
    for block_first in range(0, query_matrix.shape[1], block_rows):
        allowed = allowed_mask(seg_blk[0], block_first, block_rows)
        scores = masked_scores(
            query_matrix[0, block_first : block_first + block_rows], keys_all[0], allowed
        )
        row_peak = jnp.max(scores, axis=-1, keepdims=True)
        exp_blk = jnp.exp(scores - row_peak)
        row_total = jnp.sum(exp_blk, axis=-1, keepdims=True)
        prob_blk = (exp_blk / row_total).astype(jnp.bfloat16)
        mixed_parts.append(
            jnp.einsum(
                "hqk,khd->qhd", prob_blk, value_matrix_whole[0], preferred_element_type=jnp.float32
            ).astype(jnp.bfloat16)
        )
        log_parts.append(row_peak[..., 0] + jnp.log(row_total[..., 0]))
    return (jnp.concatenate(mixed_parts, axis=0), log_parts)


def attend_back_all(
    query_matrix, keys_all, value_matrix_whole, seg_blk, block_rows, log_parts, grad_mixed
):
    grad_q_parts = []
    position_index = 0
    grad_v_seq = jnp.zeros(value_matrix_whole.shape[1:], jnp.float32)
    for block_first in range(0, query_matrix.shape[1], block_rows):
        allowed = allowed_mask(seg_blk[0], block_first, block_rows)
        scores = masked_scores(
            query_matrix[0, block_first : block_first + block_rows], keys_all[0], allowed
        )
        prob_blk = jnp.exp(scores - log_parts[position_index][..., None])
        grad_blk = grad_mixed[0, block_first : block_first + block_rows]
        grad_probs = jnp.einsum(
            "qhd,khd->hqk", grad_blk, value_matrix_whole[0], preferred_element_type=jnp.float32
        )
        row_inner = jnp.sum(prob_blk * grad_probs, axis=-1, keepdims=True)
        grad_scores = (prob_blk * (grad_probs - row_inner)).astype(jnp.bfloat16)
        grad_query_blk = (
            jnp.einsum("hqk,khd->qhd", grad_scores, keys_all[0], preferred_element_type=jnp.float32)
            * SCORE_SCALE
        )
        grad_q_parts.append(grad_query_blk.astype(jnp.bfloat16))
        grad_v_seq = grad_v_seq + jnp.einsum(
            "hqk,qhd->khd",
            prob_blk.astype(jnp.bfloat16),
            grad_blk,
            preferred_element_type=jnp.float32,
        )
        position_index += 1
    grad_v_parts = grad_v_seq.astype(jnp.bfloat16)
    gradient_query_rows = jnp.concatenate(grad_q_parts, axis=0)
    return (
        gradient_query_rows.reshape(gradient_query_rows.shape[0], -1),
        grad_v_parts.reshape(grad_v_parts.shape[0], -1),
    )


def local(
    packed_token_rows,
    example_numbers,
    completion,
    global_token_count,
    owners,
    optimizer_step,
    embedding,
    positions,
    gains,
    query_key_value_weight,
    attention_output_weight,
    feedforward_input_weight,
    feedforward_output_weight,
    adapter_down_weight,
    adapter_up_weight,
    master,
    first_moment,
    second_moment,
):
    groups = lax.axis_size("mp")
    mp_index = lax.axis_index("mp")
    seq_len = packed_token_rows.shape[1]
    per_batch = packed_token_rows.shape[0] // MICRO
    tok_rows = per_batch * seq_len
    own_rows = tok_rows // groups
    row_start = mp_index * own_rows
    feature_width = embedding.shape[1]
    vocab_local = embedding.shape[0]
    vocab_start = mp_index * vocab_local
    head_cols = query_key_value_weight.shape[2]
    local_heads = head_cols // HEAD_DIM
    adapter_rank_size = adapter_down_weight.shape[1]
    block_rows = min(512, seq_len)
    tok_count = global_token_count.astype(jnp.float32)
    qkv_flat = query_key_value_weight.reshape(feature_width, 3 * head_cols)
    down_matrix_flat = adapter_down_weight.reshape(2 * adapter_rank_size, feature_width)
    vocab_ids = vocab_start + jnp.arange(vocab_local, dtype=jnp.int32)
    places = jnp.arange(seq_len, dtype=jnp.int32)
    split_into_heads = (per_batch, seq_len, local_heads, HEAD_DIM)
    gradient_up_matrix = jnp.zeros((2, adapter_rank_size, head_cols), jnp.float32)
    grad_down = jnp.zeros((2 * adapter_rank_size, feature_width), jnp.float32)
    loss_part = jnp.zeros((), jnp.float32)
    for batch_index in range(MICRO):
        first_seq = batch_index * per_batch
        ids_blk = packed_token_rows[first_seq : first_seq + per_batch]
        seg_blk = example_numbers[first_seq : first_seq + per_batch]
        comp_blk = completion[first_seq : first_seq + per_batch]
        ids_flat = packed_token_rows[batch_index]
        local_ids = rows_of(ids_flat, jnp.int32(0), lax.axis_size("mp") * own_rows) - vocab_start
        inside = (local_ids >= 0) & (local_ids < vocab_local)
        picked = jnp.take(embedding, jnp.clip(local_ids, 0, vocab_local - 1), axis=0)
        embedded = lax.psum_scatter(
            jnp.where(inside[:, None], picked.astype(jnp.float32), 0.0).astype(jnp.bfloat16),
            "mp",
            scatter_dimension=0,
            tiled=True,
        ).astype(jnp.float32)
        pos_index = (row_start + jnp.arange(own_rows, dtype=jnp.int32)) % seq_len
        x_zero = embedded + jnp.take(positions, pos_index, axis=0).astype(jnp.float32)
        normed_one = layer_norm(x_zero, gains[0]).astype(jnp.bfloat16)
        gathered = lax.all_gather(normed_one, "mp", axis=0, tiled=True)
        projected_query_key_value = jnp.dot(
            gathered, qkv_flat, preferred_element_type=jnp.float32
        ).reshape(tok_rows, 3, head_cols)
        reduced_rank_path = lax.dot_general(
            gathered, down_matrix_flat, CONTRACT_FINAL, preferred_element_type=jnp.float32
        ).astype(jnp.bfloat16)
        query_adapter_term = jnp.dot(
            reduced_rank_path[:, :adapter_rank_size],
            adapter_up_weight[0],
            preferred_element_type=jnp.float32,
        )
        value_adapter_term = jnp.dot(
            reduced_rank_path[:, adapter_rank_size:],
            adapter_up_weight[1],
            preferred_element_type=jnp.float32,
        )
        query_matrix = (
            (projected_query_key_value[:, 0] + ADAPTER_SCALE * query_adapter_term)
            .astype(jnp.bfloat16)
            .reshape(split_into_heads)
        )
        keys_all = projected_query_key_value[:, 1].astype(jnp.bfloat16).reshape(split_into_heads)
        value_matrix_whole = (
            (projected_query_key_value[:, 2] + ADAPTER_SCALE * value_adapter_term)
            .astype(jnp.bfloat16)
            .reshape(split_into_heads)
        )
        attn_mixed, log_parts = attend_all(
            query_matrix, keys_all, value_matrix_whole, seg_blk, block_rows
        )
        attn_mixed = attn_mixed.reshape(tok_rows, head_cols)
        hidden_one = x_zero + lax.psum_scatter(
            jnp.dot(
                rows_of(attn_mixed, jnp.int32(0), own_rows * lax.axis_size("mp")),
                attention_output_weight,
                preferred_element_type=jnp.float32,
            ),
            "mp",
            scatter_dimension=0,
            tiled=True,
        )
        normed_two = layer_norm(hidden_one, gains[1]).astype(jnp.bfloat16)
        fc_inner = jnp.dot(
            lax.all_gather(normed_two, "mp", axis=0, tiled=True),
            feedforward_input_weight,
            preferred_element_type=jnp.float32,
        )
        active = jax.nn.gelu(fc_inner, approximate=True).astype(jnp.bfloat16)
        mlp_out = lax.psum_scatter(
            lax.dot_general(
                rows_of(active, jnp.int32(0), lax.axis_size("mp") * own_rows),
                feedforward_output_weight,
                CONTRACT_FINAL,
                preferred_element_type=jnp.float32,
            ).astype(jnp.bfloat16),
            "mp",
            scatter_dimension=0,
            tiled=True,
        ).astype(jnp.float32)
        hidden_two = hidden_one + mlp_out
        final_rows = layer_norm(hidden_two, gains[2]).astype(jnp.bfloat16)
        final_all = lax.all_gather(final_rows, "mp", axis=0, tiled=True)
        targets = jnp.roll(ids_blk, -1, axis=1).reshape(-1)
        is_valid = (
            (places[None, :] < seq_len - 1)
            & (jnp.roll(seg_blk, -1, axis=1) == seg_blk)
            & (jnp.roll(comp_blk, -1, axis=1) == 1)
        )
        row_weight = is_valid.astype(jnp.float32).reshape(-1) / tok_count

        def local_stats(block_pair):
            rows_in, wanted = block_pair
            logits = lax.dot_general(
                rows_in, embedding, CONTRACT_FINAL, preferred_element_type=jnp.float32
            )
            row_peak = jnp.max(logits, axis=-1)
            row_total = jnp.sum(jnp.exp(logits - row_peak[:, None]), axis=-1)
            row_pick = jnp.sum(
                jnp.where(vocab_ids[None, :] == wanted[:, None], logits, 0.0), axis=-1
            )
            return (row_peak, row_total, row_pick)

        row_stats = lax.map(
            local_stats,
            (final_all.reshape(-1, block_rows, feature_width), targets.reshape(-1, block_rows)),
        )
        row_stats = tuple((member.reshape(-1) for member in row_stats))
        row_peak, row_total, row_pick = joined(row_stats, "mp", combine_stats)
        log_total = row_peak + jnp.log(row_total)
        token_loss = row_weight * (log_total - row_pick)
        loss_part = loss_part + jnp.sum(rows_of(token_loss, row_start, own_rows))

        def head_rows_grad(first_row, row_count):
            rows_in = rows_of(final_all, first_row, row_count)
            logits = lax.dot_general(
                rows_in, embedding, CONTRACT_FINAL, preferred_element_type=jnp.float32
            )
            prob_blk = jnp.exp(logits - rows_of(log_total, first_row, row_count)[:, None])
            onehot = (vocab_ids[None, :] == rows_of(targets, first_row, row_count)[:, None]).astype(
                jnp.float32
            )
            grad_logits = (
                (prob_blk - onehot) * rows_of(row_weight, first_row, row_count)[:, None]
            ).astype(jnp.bfloat16)
            return jnp.dot(grad_logits, embedding, preferred_element_type=jnp.float32)

        grad_final = lax.psum_scatter(
            by_blocks(head_rows_grad, lax.axis_size("mp") * own_rows, block_rows).astype(
                jnp.bfloat16
            ),
            "mp",
            scatter_dimension=0,
            tiled=True,
        ).astype(jnp.float32)
        grad_two = norm_back(hidden_two, gains[2], grad_final)
        grad_mlp = grad_two.astype(jnp.bfloat16)
        mlp_rows_in = lax.all_gather(grad_mlp, "mp", axis=0, tiled=True)
        grad_act = jnp.dot(
            mlp_rows_in, feedforward_output_weight, preferred_element_type=jnp.float32
        )
        grad_inner = gelu_back(
            rows_of(fc_inner, jnp.int32(0), mlp_rows_in.shape[0]), grad_act
        ).astype(jnp.bfloat16)
        grad_normed = lax.psum_scatter(
            lax.dot_general(
                rows_of(grad_inner, jnp.int32(0), lax.axis_size("mp") * own_rows),
                feedforward_input_weight,
                CONTRACT_FINAL,
                preferred_element_type=jnp.float32,
            ).astype(jnp.bfloat16),
            "mp",
            scatter_dimension=0,
            tiled=True,
        ).astype(jnp.float32)
        grad_one = grad_two + norm_back(hidden_one, gains[1], grad_normed)
        grad_mixed = lax.dot_general(
            lax.all_gather(grad_one.astype(jnp.bfloat16), "mp", axis=0, tiled=True),
            attention_output_weight,
            CONTRACT_FINAL,
            preferred_element_type=jnp.float32,
        ).astype(jnp.bfloat16)
        gradient_query_rows, gradient_value_rows = attend_back_all(
            query_matrix,
            keys_all,
            value_matrix_whole,
            seg_blk,
            block_rows,
            log_parts,
            grad_mixed.reshape(split_into_heads),
        )
        gradient_up_matrix = gradient_up_matrix + ADAPTER_SCALE * jnp.stack(
            [
                lax.dot_general(
                    reduced_rank_path[:, :adapter_rank_size],
                    gradient_query_rows,
                    CONTRACT_FIRST,
                    preferred_element_type=jnp.float32,
                ),
                lax.dot_general(
                    reduced_rank_path[:, adapter_rank_size:],
                    gradient_value_rows,
                    CONTRACT_FIRST,
                    preferred_element_type=jnp.float32,
                ),
            ]
        )
        gradient_reduced = ADAPTER_SCALE * jnp.concatenate(
            [
                lax.dot_general(
                    gradient_query_rows,
                    adapter_up_weight[0],
                    CONTRACT_FINAL,
                    preferred_element_type=jnp.float32,
                ),
                lax.dot_general(
                    gradient_value_rows,
                    adapter_up_weight[1],
                    CONTRACT_FINAL,
                    preferred_element_type=jnp.float32,
                ),
            ],
            axis=1,
        )
        low_own = lax.psum_scatter(
            gradient_reduced.astype(jnp.bfloat16), "mp", scatter_dimension=0, tiled=True
        )
        grad_down = grad_down + lax.dot_general(
            low_own, normed_one, CONTRACT_FIRST, preferred_element_type=jnp.float32
        )
    down_cols = grad_down.reshape(2, adapter_rank_size, groups, head_cols)
    up_onehot = (jnp.arange(groups, dtype=jnp.int32) == mp_index).astype(jnp.float32)
    up_cols = up_onehot[None, None, :, None] * gradient_up_matrix[:, :, None, :]
    all_cols = jnp.concatenate([down_cols, up_cols], axis=0)
    dp_size = lax.axis_size("dp")
    owner_slots = (
        owners[None, :, :] == jnp.arange(dp_size, dtype=jnp.int32)[:, None, None]
    ).astype(jnp.float32)
    my_slots = lax.dynamic_index_in_dim(owner_slots, lax.axis_index("dp"), 0, keepdims=False)
    buffer = owner_slots[:, None, :, :, None] * jnp.transpose(all_cols, (2, 0, 1, 3))[None]
    owned = lax.psum_scatter(
        buffer.reshape(dp_size * groups, 4, adapter_rank_size, head_cols),
        ("dp", "mp"),
        scatter_dimension=0,
        tiled=True,
    )[0]
    square_sum, completion_loss = lax.psum((jnp.sum(owned * owned), loss_part), ("dp", "mp"))
    grad_norm = jnp.sqrt(square_sum)
    clipped = owned * jnp.minimum(1.0, CLIP_NORM / (grad_norm + 1e-06))
    new_first = BETA_ONE * first_moment + (1.0 - BETA_ONE) * clipped
    new_second = BETA_TWO * second_moment + (1.0 - BETA_TWO) * clipped * clipped
    step_float = optimizer_step.astype(jnp.float32)
    first_hat = new_first / (1.0 - jnp.power(BETA_ONE, step_float))
    second_hat = new_second / (1.0 - jnp.power(BETA_TWO, step_float))
    new_weight = master - LEARN_RATE * (
        first_hat / (jnp.sqrt(second_hat) + ADAM_EPS) + WEIGHT_DECAY * master
    )
    slot_mask = my_slots[None, :, :, None]
    return (
        completion_loss,
        grad_norm,
        slot_mask * new_first[None],
        slot_mask * new_second[None],
        slot_mask * new_weight[None],
        (slot_mask * new_weight[None]).astype(jnp.bfloat16),
    )


def solution(mesh):
    return jax.shard_map(
        local,
        mesh=mesh,
        in_specs=(
            P("dp", None),
            P("dp", None),
            P("dp", None),
            P(),
            P(),
            P(),
            P("mp", None),
            P(),
            P(),
            P(None, None, "mp"),
            P("mp", None),
            P(None, "mp"),
            P(None, "mp"),
            P(),
            P(None, None, "mp"),
            P(None, None, "mp"),
            P(None, None, "mp"),
            P(None, None, "mp"),
        ),
        out_specs=(
            P(),
            P(),
            P("dp", None, None, "mp"),
            P("dp", None, None, "mp"),
            P("dp", None, None, "mp"),
            P("dp", None, None, "mp"),
        ),
        check_vma=False,
    )
```

profile of v0, /device:TPU:0, one launch (start us, length us, event | category | flops | bytes accessed | tf_op | source)
XLA Modules:
  0.0 3450.1 jit_solution(10644205049073891520)
XLA Ops:
  96.0 71.0 %reduce-scatter.51.cloned.1.call-done = bf16[128,1024]{1,0:T(8,128)(2,1)} async-done(((bf16[1024,1024]{1,0:T(8,128)(2,1)}), bf16[128,1024]{1,0:T(8,128)(2,1)}) %reduce-scatter.51.cloned.1.call-update) | async-done | bytes 262160 | tf_op jit(solution)/shard_map/reduce_scatter | solution.py:192
  168.3 69.6 %reduce-scatter.39.cloned.1.call-done = bf16[128,1024]{1,0:T(8,128)(2,1)} async-done(((bf16[1024,1024]{1,0:T(8,128)(2,1)}), bf16[128,1024]{1,0:T(8,128)(2,1)}) %reduce-scatter.39.cloned.1.call-update) | async-done | bytes 262160 | tf_op jit(solution)/shard_map/reduce_scatter | solution.py:192
  238.0 71.0 %reduce-scatter.45.cloned.1.call-done = bf16[128,1024]{1,0:T(8,128)(2,1)} async-done(((bf16[1024,1024]{1,0:T(8,128)(2,1)}), bf16[128,1024]{1,0:T(8,128)(2,1)}) %reduce-scatter.45.cloned.1.call-update) | async-done | bytes 262160 | tf_op jit(solution)/shard_map/reduce_scatter | solution.py:192
  318.7 44.3 %all-gather.45.cloned.1.call-done = bf16[1024,1024]{1,0:T(8,128)(2,1)} async-done(((bf16[128,1024]{1,0:T(8,128)(2,1)}), bf16[1024,1024]{1,0:T(8,128)(2,1)}) %all-gather.45.cloned.1.call-update) | async-done | bytes 2097168 | tf_op jit(solution)/shard_map/all_gather | solution.py:201
  378.5 34.2 all-gather.33.cloned.1.call-done
  427.5 34.9 %all-gather.39.cloned.1.call-done = bf16[1024,1024]{1,0:T(8,128)(2,1)} async-done(((bf16[128,1024]{1,0:T(8,128)(2,1)}), bf16[1024,1024]{1,0:T(8,128)(2,1)}) %all-gather.39.cloned.1.call-update) | async-done | bytes 2097168 | tf_op jit(solution)/shard_map/all_gather | solution.py:201
  477.4 34.8 %all-gather.51.cloned.1.call-done = bf16[1024,1024]{1,0:T(8,128)(2,1)} async-done(((bf16[128,1024]{1,0:T(8,128)(2,1)}), bf16[1024,1024]{1,0:T(8,128)(2,1)}) %all-gather.51.cloned.1.call-update) | async-done | bytes 2097168 | tf_op jit(solution)/shard_map/all_gather | solution.py:201
  525.7 77.0 %reduce-scatter.47.cloned.1.call-done = f32[128,1024]{1,0:T(8,128)} async-done(((f32[1024,1024]{1,0:T(8,128)}), f32[128,1024]{1,0:T(8,128)}) %reduce-scatter.47.cloned.1.call-update) | async-done | bytes 524304 | tf_op jit(solution)/shard_map/reduce_scatter | solution.py:233
  602.7 91.4 %reduce-scatter.35.cloned.1.call-done = f32[128,1024]{1,0:T(8,128)} async-done(((f32[1024,1024]{1,0:T(8,128)}), f32[128,1024]{1,0:T(8,128)}) %reduce-scatter.35.cloned.1.call-update) | async-done | bytes 524304 | tf_op jit(solution)/shard_map/reduce_scatter | solution.py:233
  694.1 91.7 %reduce-scatter.41.cloned.1.call-done = f32[128,1024]{1,0:T(8,128)} async-done(((f32[1024,1024]{1,0:T(8,128)}), f32[128,1024]{1,0:T(8,128)}) %reduce-scatter.41.cloned.1.call-update) | async-done | bytes 524304 | tf_op jit(solution)/shard_map/reduce_scatter | solution.py:233
  785.8 91.5 %reduce-scatter.53.cloned.1.call-done = f32[128,1024]{1,0:T(8,128)} async-done(((f32[1024,1024]{1,0:T(8,128)}), f32[128,1024]{1,0:T(8,128)}) %reduce-scatter.53.cloned.1.call-update) | async-done | bytes 524304 | tf_op jit(solution)/shard_map/reduce_scatter | solution.py:233
  885.5 46.7 %all-gather.35.cloned.1.call-done = bf16[1024,1024]{1,0:T(8,128)(2,1)} async-done(((bf16[128,1024]{1,0:T(8,128)(2,1)}), bf16[1024,1024]{1,0:T(8,128)(2,1)}) %all-gather.35.cloned.1.call-update) | async-done | bytes 2097168 | tf_op jit(solution)/shard_map/all_gather | solution.py:245
  939.4 42.4 %all-gather.47.cloned.1.call-done = bf16[1024,1024]{1,0:T(8,128)(2,1)} async-done(((bf16[128,1024]{1,0:T(8,128)(2,1)}), bf16[1024,1024]{1,0:T(8,128)(2,1)}) %all-gather.47.cloned.1.call-update) | async-done | bytes 2097168 | tf_op jit(solution)/shard_map/all_gather | solution.py:245
  989.1 42.4 %all-gather.41.cloned.1.call-done = bf16[1024,1024]{1,0:T(8,128)(2,1)} async-done(((bf16[128,1024]{1,0:T(8,128)(2,1)}), bf16[1024,1024]{1,0:T(8,128)(2,1)}) %all-gather.41.cloned.1.call-update) | async-done | bytes 2097168 | tf_op jit(solution)/shard_map/all_gather | solution.py:245
  1038.8 42.3 %all-gather.53.cloned.1.call-done = bf16[1024,1024]{1,0:T(8,128)(2,1)} async-done(((bf16[128,1024]{1,0:T(8,128)(2,1)}), bf16[1024,1024]{1,0:T(8,128)(2,1)}) %all-gather.53.cloned.1.call-update) | async-done | bytes 2097168 | tf_op jit(solution)/shard_map/all_gather | solution.py:245
  1088.3 63.2 %reduce-scatter.37.cloned.1.call-done = bf16[128,1024]{1,0:T(8,128)(2,1)} async-done(((bf16[1024,1024]{1,0:T(8,128)(2,1)}), bf16[128,1024]{1,0:T(8,128)(2,1)}) %reduce-scatter.37.cloned.1.call-update) | async-done | bytes 262160 | tf_op jit(solution)/shard_map/reduce_scatter | solution.py:250
  1152.7 69.5 %reduce-scatter.49.cloned.1.call-done = bf16[128,1024]{1,0:T(8,128)(2,1)} async-done(((bf16[1024,1024]{1,0:T(8,128)(2,1)}), bf16[128,1024]{1,0:T(8,128)(2,1)}) %reduce-scatter.49.cloned.1.call-update) | async-done | bytes 262160 | tf_op jit(solution)/shard_map/reduce_scatter | solution.py:250
  1223.4 69.7 %reduce-scatter.43.cloned.1.call-done = bf16[128,1024]{1,0:T(8,128)(2,1)} async-done(((bf16[1024,1024]{1,0:T(8,128)(2,1)}), bf16[128,1024]{1,0:T(8,128)(2,1)}) %reduce-scatter.43.cloned.1.call-update) | async-done | bytes 262160 | tf_op jit(solution)/shard_map/reduce_scatter | solution.py:250
  1298.4 65.6 %reduce-scatter.55.cloned.1.call-done = bf16[128,1024]{1,0:T(8,128)(2,1)} async-done(((bf16[1024,1024]{1,0:T(8,128)(2,1)}), bf16[128,1024]{1,0:T(8,128)(2,1)}) %reduce-scatter.55.cloned.1.call-update) | async-done | bytes 262160 | tf_op jit(solution)/shard_map/reduce_scatter | solution.py:250
  1385.4 31.5 all-gather.37.cloned.1.call-done
  1417.0 44.5 %while.184 = (s32[]{:T(128)}, f32[2,512]{1,0:T(2,128)S(1)}, f32[2,512]{1,0:T(2,128)S(1)}, f32[2,512]{1,0:T(2,128)S(1)}, bf16[2,512,1024]{2,1,0:T(8,128)(2,1)}, /...) while((s32[]{:T(128)}, f32[2,512]{1,0:T(2,128)S(1)}, ...), condition=%wide.region_17.20_spmd.clone, body=%wide.region_13.19_spmd.clone.sunk | while | flops 6730552320 | bytes 40448632 | solution.py:284
  1492.4 31.3 all-gather.1
  1523.7 31.0 all-gather.2
  1554.8 44.5 %while.185 = (s32[]{:T(128)}, f32[2,512]{1,0:T(2,128)S(1)}, f32[2,512]{1,0:T(2,128)S(1)}, f32[2,512]{1,0:T(2,128)S(1)}, bf16[2,512,1024]{2,1,0:T(8,128)(2,1)}, /...) while((s32[]{:T(128)}, f32[2,512]{1,0:T(2,128)S(1)}, ...), condition=%wide.region_38.41_spmd.clone, body=%wide.region_34.40_spmd.clone.sunk | while | flops 6730552320 | bytes 40448632 | solution.py:284
  1694.9 53.9 %while.188 = (s32[]{:T(128)}, bf16[2,512,1024]{2,1,0:T(8,128)(2,1)S(1)}, s32[2]{0:T(128)S(1)}, bf16[1024,1024]{1,0:T(8,128)(2,1)}, bf16[6400,1024]{1,0:T(8,128)(...) while((s32[]{:T(128)}, ...), condition=%wide.region_86.89_spmd.clone, body=%wide.region_85.88_spmd.clone.sunk | while | flops 13441439744 | bytes 29433528 | solution.py:54
  1762.4 55.7 %while.189 = (s32[]{:T(128)}, bf16[2,512,1024]{2,1,0:T(8,128)(2,1)}, s32[2]{0:T(128)S(1)}, bf16[1024,1024]{1,0:T(8,128)(2,1)}, bf16[6400,1024]{1,0:T(8,128)(2,1)...) while((s32[]{:T(128)}, bf16[2,512,1024]{2,1,0:T(8,128)(2,1)}, ...), condition=%wide.region_97.100_spmd.clone, body=%wide.region_96.99_spmd.clone.sunk | while | flops 13441439744 | bytes 29430456 | solution.py:54
  1818.1 44.8 %while.186 = (s32[]{:T(128)}, f32[2,512]{1,0:T(2,128)S(1)}, f32[2,512]{1,0:T(2,128)S(1)}, f32[2,512]{1,0:T(2,128)S(1)}, bf16[2,512,1024]{2,1,0:T(8,128)(2,1)}, /...) while((s32[]{:T(128)}, f32[2,512]{1,0:T(2,128)S(1)}, ...), condition=%wide.region_59.62_spmd.clone, body=%wide.region_55.61_spmd.clone.sunk | while | flops 6730552320 | bytes 40448632 | solution.py:284
  1956.4 53.9 %while.190 = (s32[]{:T(128)}, bf16[2,512,1024]{2,1,0:T(8,128)(2,1)S(1)}, s32[2]{0:T(128)S(1)}, bf16[1024,1024]{1,0:T(8,128)(2,1)}, bf16[6400,1024]{1,0:T(8,128)(...) while((s32[]{:T(128)}, ...), condition=%wide.region_108.111_spmd.clone, body=%wide.region_107.110_spmd.clone.sunk | while | flops 13441439744 | bytes 29433528 | solution.py:54
  2011.7 44.8 %while.187 = (s32[]{:T(128)}, f32[2,512]{1,0:T(2,128)S(1)}, f32[2,512]{1,0:T(2,128)S(1)}, f32[2,512]{1,0:T(2,128)S(1)}, bf16[2,512,1024]{2,1,0:T(8,128)(2,1)}, /...) while((s32[]{:T(128)}, f32[2,512]{1,0:T(2,128)S(1)}, ...), condition=%wide.region_80.83_spmd.clone, body=%wide.region_76.82_spmd.clone.sunk | while | flops 6730552320 | bytes 40448632 | solution.py:284
  2151.7 55.9 %while.191 = (s32[]{:T(128)}, bf16[2,512,1024]{2,1,0:T(8,128)(2,1)}, s32[2]{0:T(128)S(1)}, bf16[1024,1024]{1,0:T(8,128)(2,1)}, bf16[6400,1024]{1,0:T(8,128)(2,1)...) while((s32[]{:T(128)}, bf16[2,512,1024]{2,1,0:T(8,128)(2,1)}, ...), condition=%wide.region_119.122_spmd.clone, body=%wide.region_118.121_spmd.clone.sunk | while | flops 13441439744 | bytes 29430456 | solution.py:54
  2215.8 70.9 %reduce-scatter.69.cloned.1.call-done = bf16[128,1024]{1,0:T(8,128)(2,1)} async-done(((bf16[1024,1024]{1,0:T(8,128)(2,1)}), bf16[128,1024]{1,0:T(8,128)(2,1)}) %reduce-scatter.69.cloned.1.call-update) | async-done | bytes 262160 | tf_op jit(solution)/shard_map/reduce_scatter | solution.py:308
  2297.7 42.3 %all-gather.65.cloned.1.call-done = bf16[1024,1024]{1,0:T(8,128)(2,1)} async-done(((bf16[128,1024]{1,0:T(8,128)(2,1)}), bf16[1024,1024]{1,0:T(8,128)(2,1)}) %all-gather.65.cloned.1.call-update) | async-done | bytes 2097168 | tf_op jit(solution)/shard_map/all_gather | solution.py:318
  2347.5 42.1 %all-gather.57.cloned.1.call-done = bf16[1024,1024]{1,0:T(8,128)(2,1)} async-done(((bf16[128,1024]{1,0:T(8,128)(2,1)}), bf16[1024,1024]{1,0:T(8,128)(2,1)}) %all-gather.57.cloned.1.call-update) | async-done | bytes 2097168 | tf_op jit(solution)/shard_map/all_gather | solution.py:318
  2397.1 42.2 %all-gather.61.cloned.1.call-done = bf16[1024,1024]{1,0:T(8,128)(2,1)} async-done(((bf16[128,1024]{1,0:T(8,128)(2,1)}), bf16[1024,1024]{1,0:T(8,128)(2,1)}) %all-gather.61.cloned.1.call-update) | async-done | bytes 2097168 | tf_op jit(solution)/shard_map/all_gather | solution.py:318
  2447.3 41.8 %all-gather.69.cloned.1.call-done = bf16[1024,1024]{1,0:T(8,128)(2,1)} async-done(((bf16[128,1024]{1,0:T(8,128)(2,1)}), bf16[1024,1024]{1,0:T(8,128)(2,1)}) %all-gather.69.cloned.1.call-update) | async-done | bytes 2097168 | tf_op jit(solution)/shard_map/all_gather | solution.py:318
  2496.7 62.7 %reduce-scatter.67.cloned.1.call-done = bf16[128,1024]{1,0:T(8,128)(2,1)} async-done(((bf16[1024,1024]{1,0:T(8,128)(2,1)}), bf16[128,1024]{1,0:T(8,128)(2,1)}) %reduce-scatter.67.cloned.1.call-update) | async-done | bytes 262160 | tf_op jit(solution)/shard_map/reduce_scatter | solution.py:325
  2560.7 69.6 %reduce-scatter.59.cloned.1.call-done = bf16[128,1024]{1,0:T(8,128)(2,1)} async-done(((bf16[1024,1024]{1,0:T(8,128)(2,1)}), bf16[128,1024]{1,0:T(8,128)(2,1)}) %reduce-scatter.59.cloned.1.call-update) | async-done | bytes 262160 | tf_op jit(solution)/shard_map/reduce_scatter | solution.py:325
  2630.4 70.9 %reduce-scatter.63.cloned.1.call-done = bf16[128,1024]{1,0:T(8,128)(2,1)} async-done(((bf16[1024,1024]{1,0:T(8,128)(2,1)}), bf16[128,1024]{1,0:T(8,128)(2,1)}) %reduce-scatter.63.cloned.1.call-update) | async-done | bytes 262160 | tf_op jit(solution)/shard_map/reduce_scatter | solution.py:325
  2701.2 70.8 %reduce-scatter.71.cloned.1.call-done = bf16[128,1024]{1,0:T(8,128)(2,1)} async-done(((bf16[1024,1024]{1,0:T(8,128)(2,1)}), bf16[128,1024]{1,0:T(8,128)(2,1)}) %reduce-scatter.71.cloned.1.call-update) | async-done | bytes 262160 | tf_op jit(solution)/shard_map/reduce_scatter | solution.py:325
  2781.2 44.2 %all-gather.71.cloned.1.call-done = bf16[1024,1024]{1,0:T(8,128)(2,1)} async-done(((bf16[128,1024]{1,0:T(8,128)(2,1)}), bf16[1024,1024]{1,0:T(8,128)(2,1)}) %all-gather.71.cloned.1.call-update) | async-done | bytes 2097168 | tf_op jit(solution)/shard_map/all_gather | solution.py:338
  2827.8 47.3 %all-gather.67.cloned.1.call-done = bf16[1024,1024]{1,0:T(8,128)(2,1)} async-done(((bf16[128,1024]{1,0:T(8,128)(2,1)}), bf16[1024,1024]{1,0:T(8,128)(2,1)}) %all-gather.67.cloned.1.call-update) | async-done | bytes 2097168 | tf_op jit(solution)/shard_map/all_gather | solution.py:338
  2877.6 47.2 %all-gather.63.cloned.1.call-done = bf16[1024,1024]{1,0:T(8,128)(2,1)} async-done(((bf16[128,1024]{1,0:T(8,128)(2,1)}), bf16[1024,1024]{1,0:T(8,128)(2,1)}) %all-gather.63.cloned.1.call-update) | async-done | bytes 2097168 | tf_op jit(solution)/shard_map/all_gather | solution.py:338
  3017.1 57.8 %reduce-scatter.73.cloned.1.call-done = bf16[128,8]{1,0:T(8,128)(2,1)} async-done(((bf16[1024,8]{1,0:T(8,128)(2,1)}), bf16[128,8]{1,0:T(8,128)(2,1)}) %reduce-scatter.73.cloned.1.call-update) | async-done | bytes 2064
  3075.9 63.6 %reduce-scatter.75.cloned.1.call-done = bf16[128,8]{1,0:T(8,128)(2,1)} async-done(((bf16[1024,8]{1,0:T(8,128)(2,1)}), bf16[128,8]{1,0:T(8,128)(2,1)}) %reduce-scatter.75.cloned.1.call-update) | async-done | bytes 2064
  3140.4 63.4 %reduce-scatter.77.cloned.1.call-done = bf16[128,8]{1,0:T(8,128)(2,1)} async-done(((bf16[1024,8]{1,0:T(8,128)(2,1)}), bf16[128,8]{1,0:T(8,128)(2,1)}) %reduce-scatter.77.cloned.1.call-update) | async-done | bytes 2064
  3204.8 63.6 %reduce-scatter.79.cloned.1.call-done = bf16[128,8]{1,0:T(8,128)(2,1)} async-done(((bf16[1024,8]{1,0:T(8,128)(2,1)}), bf16[128,8]{1,0:T(8,128)(2,1)}) %reduce-scatter.79.cloned.1.call-update) | async-done | bytes 2064
  3279.2 120.1 %all-reduce.4.cloned.1.call-done = f32[32,4,4,128]{3,2,1,0:T(4,128)} async-done(((f32[32,4,4,128]{3,2,1,0:T(4,128)}), f32[32,4,4,128]{3,2,1,0:T(4,128)}) %all-reduce.4.cloned.1.call-update) | async-done | bytes 262160
  3400.6 39.5 %all-reduce.1 = (f32[]{:T(128)}, f32[]{:T(128)}) all-reduce(f32[]{:T(128)S(6)} %add.819, f32[]{:T(128)} %multiply_reduce_fusion.28), channel_id=1, replica_groups=mesh['dp'=4,'mp'=8] {'dp','mp'}, use_global_device_ids=true, to_apply=%region_84.87 | all-reduce | flops 2 | bytes 16 | tf_op jit(solution)/shard_map/psum | solution.py:407
  (1057 shorter events, 1114.4 us)
Async XLA Ops:
  7.2 88.9 %reduce-scatter.33.cloned.1.call-start = ((), (), s32[]{:S(2)}) async-start(), calls=%async_computation.24 | async-start | bytes 2359296 | tf_op jit(solution)/shard_map/reduce_scatter | solution.py:192
  24.8 142.2 %reduce-scatter.51.cloned.1.call-start = ((), (), s32[]{:S(2)}) async-start(), calls=%async_computation.42 | async-start | bytes 2359296 | tf_op jit(solution)/shard_map/reduce_scatter | solution.py:192
  40.6 197.4 %reduce-scatter.39.cloned.1.call-start = ((), (), s32[]{:S(2)}) async-start(), calls=%async_computation.30 | async-start | bytes 2359296 | tf_op jit(solution)/shard_map/reduce_scatter | solution.py:192
  56.5 252.5 %reduce-scatter.45.cloned.1.call-start = ((), (), s32[]{:S(2)}) async-start(), calls=%async_computation.36 | async-start | bytes 2359296 | tf_op jit(solution)/shard_map/reduce_scatter | solution.py:192
  72.6 290.4 %all-gather.45.cloned.1.call-start = ((), (), s32[]{:S(2)}) async-start(), calls=%async_computation.37 | async-start | bytes 2359296 | tf_op jit(solution)/shard_map/all_gather | solution.py:201
  73.6 808.3 %copy-start.93 = (f32[1,1024]{1,0:T(1,128)}, f32[1,1024]{1,0:T(1,128)S(1)}, u32[]{:S(2)}) copy-start(f32[1,1024]{1,0:T(1,128)S(1)} %get-tuple-element.1606) | copy-start | bytes 12292
  73.7 1292.6 %copy-start.101 = (f32[1,1024]{1,0:T(1,128)}, f32[1,1024]{1,0:T(1,128)S(1)}, u32[]{:S(2)}) copy-start(f32[1,1024]{1,0:T(1,128)S(1)} %get-tuple-element.1608) | copy-start | bytes 12292
  314.8 97.9 %all-gather.33.cloned.1.call-start = ((), (), s32[]{:S(2)}) async-start(), calls=%async_computation.25 | async-start | bytes 2359296 | tf_op jit(solution)/shard_map/all_gather | solution.py:201
  315.4 147.1 %all-gather.39.cloned.1.call-start = ((), (), s32[]{:S(2)}) async-start(), calls=%async_computation.31 | async-start | bytes 2359296 | tf_op jit(solution)/shard_map/all_gather | solution.py:201
  316.1 196.1 %all-gather.51.cloned.1.call-start = ((), (), s32[]{:S(2)}) async-start(), calls=%async_computation.43 | async-start | bytes 2359296 | tf_op jit(solution)/shard_map/all_gather | solution.py:201
  318.4 284.2 %reduce-scatter.47.cloned.1.call-start = ((), (), s32[]{:S(2)}) async-start(), calls=%async_computation.38 | async-start | bytes 4718592 | tf_op jit(solution)/shard_map/reduce_scatter | solution.py:233
  376.8 317.3 %reduce-scatter.35.cloned.1.call-start = ((), (), s32[]{:S(2)}) async-start(), calls=%async_computation.26 | async-start | bytes 4718592 | tf_op jit(solution)/shard_map/reduce_scatter | solution.py:233
  426.2 359.6 %reduce-scatter.41.cloned.1.call-start = ((), (), s32[]{:S(2)}) async-start(), calls=%async_computation.32 | async-start | bytes 4718592 | tf_op jit(solution)/shard_map/reduce_scatter | solution.py:233
  476.0 401.2 %reduce-scatter.53.cloned.1.call-start = ((), (), s32[]{:S(2)}) async-start(), calls=%async_computation.44 | async-start | bytes 4718592 | tf_op jit(solution)/shard_map/reduce_scatter | solution.py:233
  525.6 406.6 %all-gather.35.cloned.1.call-start = ((), (), s32[]{:S(2)}) async-start(), calls=%async_computation.27 | async-start | bytes 2359296 | tf_op jit(solution)/shard_map/all_gather | solution.py:245
  879.3 487.0 %copy-start.23 = (f32[128,1024]{1,0:T(8,128)}, f32[128,1024]{1,0:T(8,128)S(1)}, u32[]{:S(2)}) copy-start(f32[128,1024]{1,0:T(8,128)S(1)} %get-tuple-element.1564) | copy-start | bytes 1572868
  883.3 98.5 %all-gather.47.cloned.1.call-start = ((), (), s32[]{:S(2)}) async-start(), calls=%async_computation.39 | async-start | bytes 2359296 | tf_op jit(solution)/shard_map/all_gather | solution.py:245
  883.9 147.6 %all-gather.41.cloned.1.call-start = ((), (), s32[]{:S(2)}) async-start(), calls=%async_computation.33 | async-start | bytes 2359296 | tf_op jit(solution)/shard_map/all_gather | solution.py:245
  884.5 196.6 %all-gather.53.cloned.1.call-start = ((), (), s32[]{:S(2)}) async-start(), calls=%async_computation.45 | async-start | bytes 2359296 | tf_op jit(solution)/shard_map/all_gather | solution.py:245
  885.1 266.5 %reduce-scatter.37.cloned.1.call-start = ((), (), s32[]{:S(2)}) async-start(), calls=%async_computation.28 | async-start | bytes 2359296 | tf_op jit(solution)/shard_map/reduce_scatter | solution.py:250
  939.4 282.9 %reduce-scatter.49.cloned.1.call-start = ((), (), s32[]{:S(2)}) async-start(), calls=%async_computation.40 | async-start | bytes 2359296 | tf_op jit(solution)/shard_map/reduce_scatter | solution.py:250
  989.0 304.1 %reduce-scatter.43.cloned.1.call-start = ((), (), s32[]{:S(2)}) async-start(), calls=%async_computation.34 | async-start | bytes 2359296 | tf_op jit(solution)/shard_map/reduce_scatter | solution.py:250
  1038.7 325.2 %reduce-scatter.55.cloned.1.call-start = ((), (), s32[]{:S(2)}) async-start(), calls=%async_computation.46 | async-start | bytes 2359296 | tf_op jit(solution)/shard_map/reduce_scatter | solution.py:250
  1088.3 328.7 %all-gather.37.cloned.1.call-start = ((), (), s32[]{:S(2)}) async-start(), calls=%async_computation.29 | async-start | bytes 2359296 | tf_op jit(solution)/shard_map/all_gather | solution.py:263
  1368.6 186.2 %all-gather.43.cloned.1.call-start = ((), (), s32[]{:S(2)}) async-start(), calls=%async_computation.35 | async-start | bytes 2359296 | tf_op jit(solution)/shard_map/all_gather | solution.py:263
  1369.4 448.6 %all-gather.49.cloned.1.call-start = ((), (), s32[]{:S(2)}) async-start(), calls=%async_computation.41 | async-start | bytes 2359296 | tf_op jit(solution)/shard_map/all_gather | solution.py:263
  1370.2 640.3 %all-gather.55.cloned.1.call-start = ((), (), s32[]{:S(2)}) async-start(), calls=%async_computation.47 | async-start | bytes 2359296 | tf_op jit(solution)/shard_map/all_gather | solution.py:263
  1385.2 822.8 %reduce-scatter.57.cloned.1.call-start = ((), (), s32[]{:S(2)}) async-start(), calls=%async_computation.48 | async-start | bytes 2359296 | tf_op jit(solution)/shard_map/reduce_scatter | solution.py:308
  1955.5 252.5 %reduce-scatter.61.cloned.1.call-start = ((), (), s32[]{:S(2)}) async-start(), calls=%async_computation.52 | async-start | bytes 2359296 | tf_op jit(solution)/shard_map/reduce_scatter | solution.py:308
  2010.4 205.4 %reduce-scatter.65.cloned.1.call-start = ((), (), s32[]{:S(2)}) async-start(), calls=%async_computation.56 | async-start | bytes 2359296 | tf_op jit(solution)/shard_map/reduce_scatter | solution.py:308
  2149.4 137.3 %reduce-scatter.69.cloned.1.call-start = ((), (), s32[]{:S(2)}) async-start(), calls=%async_computation.60 | async-start | bytes 2359296 | tf_op jit(solution)/shard_map/reduce_scatter | solution.py:308
  2207.7 132.2 %all-gather.65.cloned.1.call-start = ((), (), s32[]{:S(2)}) async-start(), calls=%async_computation.57 | async-start | bytes 2359296 | tf_op jit(solution)/shard_map/all_gather | solution.py:318
  2291.6 98.0 %all-gather.57.cloned.1.call-start = ((), (), s32[]{:S(2)}) async-start(), calls=%async_computation.49 | async-start | bytes 2359296 | tf_op jit(solution)/shard_map/all_gather | solution.py:318
  2294.8 144.6 %all-gather.61.cloned.1.call-start = ((), (), s32[]{:S(2)}) async-start(), calls=%async_computation.53 | async-start | bytes 2359296 | tf_op jit(solution)/shard_map/all_gather | solution.py:318
  2295.7 193.5 %all-gather.69.cloned.1.call-start = ((), (), s32[]{:S(2)}) async-start(), calls=%async_computation.61 | async-start | bytes 2359296 | tf_op jit(solution)/shard_map/all_gather | solution.py:318
  2297.6 261.9 %reduce-scatter.67.cloned.1.call-start = ((), (), s32[]{:S(2)}) async-start(), calls=%async_computation.58 | async-start | bytes 2359296 | tf_op jit(solution)/shard_map/reduce_scatter | solution.py:325
  2347.4 282.9 %reduce-scatter.59.cloned.1.call-start = ((), (), s32[]{:S(2)}) async-start(), calls=%async_computation.50 | async-start | bytes 2359296 | tf_op jit(solution)/shard_map/reduce_scatter | solution.py:325
  2397.1 304.1 %reduce-scatter.63.cloned.1.call-start = ((), (), s32[]{:S(2)}) async-start(), calls=%async_computation.54 | async-start | bytes 2359296 | tf_op jit(solution)/shard_map/reduce_scatter | solution.py:325
  2446.9 325.1 %reduce-scatter.71.cloned.1.call-start = ((), (), s32[]{:S(2)}) async-start(), calls=%async_computation.62 | async-start | bytes 2359296 | tf_op jit(solution)/shard_map/reduce_scatter | solution.py:325
  2496.7 328.7 %all-gather.71.cloned.1.call-start = ((), (), s32[]{:S(2)}) async-start(), calls=%async_computation.63 | async-start | bytes 2359296 | tf_op jit(solution)/shard_map/all_gather | solution.py:338
  2777.2 98.0 %all-gather.67.cloned.1.call-start = ((), (), s32[]{:S(2)}) async-start(), calls=%async_computation.59 | async-start | bytes 2359296 | tf_op jit(solution)/shard_map/all_gather | solution.py:338
  2777.9 146.9 %all-gather.63.cloned.1.call-start = ((), (), s32[]{:S(2)}) async-start(), calls=%async_computation.55 | async-start | bytes 2359296 | tf_op jit(solution)/shard_map/all_gather | solution.py:338
  2780.3 194.3 %all-gather.59.cloned.1.call-start = ((), (), s32[]{:S(2)}) async-start(), calls=%async_computation.51 | async-start | bytes 2359296 | tf_op jit(solution)/shard_map/all_gather | solution.py:338
  2781.1 293.8 %reduce-scatter.73.cloned.1.call-start = ((), (), s32[]{:S(2)}) async-start(), calls=%async_computation.64 | async-start | bytes 294912
  3014.1 125.3 %reduce-scatter.75.cloned.1.call-start = ((), (), s32[]{:S(2)}) async-start(), calls=%async_computation.65 | async-start | bytes 294912
  3015.1 188.7 %reduce-scatter.77.cloned.1.call-start = ((), (), s32[]{:S(2)}) async-start(), calls=%async_computation.66 | async-start | bytes 294912
  3016.0 252.3 %reduce-scatter.79.cloned.1.call-start = ((), (), s32[]{:S(2)}) async-start(), calls=%async_computation.67 | async-start | bytes 294912
  3017.0 382.3 %all-reduce.4.cloned.1.call-start = ((), (), s32[]{:S(2)}) async-start(), calls=%async_computation.68 | async-start | bytes 524288
  (203 other events, 14438.8 us)
Sparse Core Ops, SparseCore 0:
  24.9 71.0 reduce-scatter.32
  99.6 67.3 reduce-scatter.50
  170.5 67.3 reduce-scatter.38
  241.3 67.5 reduce-scatter.44
  314.9 48.0 all-gather.44
  365.0 47.6 all-gather.32
  414.8 47.5 all-gather.38
  464.6 47.5 all-gather.50
  515.8 86.8 reduce-scatter.46
  606.2 87.8 reduce-scatter.34
  697.7 87.9 reduce-scatter.40
  789.2 87.9 reduce-scatter.52
  883.5 48.7 all-gather.34
  934.2 47.6 all-gather.46
  983.8 47.6 all-gather.40
  1033.4 47.6 all-gather.52
  1084.5 67.0 reduce-scatter.36
  1155.0 67.2 reduce-scatter.48
  1225.8 67.2 reduce-scatter.42
  1296.5 67.4 reduce-scatter.54
  1368.8 48.1 all-gather.36
  1419.1 47.6 all-gather.42
  1469.0 48.0 all-gather.48
  1519.1 47.9 all-gather.54
  1955.6 66.3 reduce-scatter.56
  2025.4 67.4 reduce-scatter.60
  2149.5 66.2 reduce-scatter.64
  2219.4 67.2 reduce-scatter.68
  2291.7 48.1 all-gather.64
  2341.9 47.6 all-gather.56
  2391.7 47.6 all-gather.60
  2441.5 47.6 all-gather.68
  2492.5 66.9 reduce-scatter.66
  2563.0 67.2 reduce-scatter.58
  2633.9 67.2 reduce-scatter.62
  2704.6 67.3 reduce-scatter.70
  2777.3 48.0 all-gather.70
  2827.5 47.6 all-gather.66
  2877.1 47.6 all-gather.62
  2926.9 47.6 all-gather.58
  3014.3 60.6 reduce-scatter.72
  3078.3 61.1 reduce-scatter.74
  3142.6 61.1 reduce-scatter.76
  3207.1 61.1 reduce-scatter.78
  3273.7 125.5 all-reduce.3
where the time goes:
time: 3460 us; the launch traced here: 3450 us
  waiting for transfers between devices  2270 us (66%)
  matrix products  469 us (14%)
  blocking collectives  408 us (12%)
  other arithmetic  148 us (4%)
  local copies, waits for them, and re-layouts  106 us (3%)
    unnamed x50, waiting for transfers between devices  374 us
    all_gather x12, blocking collectives, joined(): everything = jax.tree.map(lambda part: lax.all_gather(part, axis), shard)  369 us
    reduce_scatter x4, waiting for transfers between devices, local(): lax.psum_scatter(jnp.dot(rows_of(attn_mixed, jnp.int32(0), own_rows * lax...  352 us
    reduce_scatter x4, waiting for transfers between devices, local(): lax.psum_scatter(lax.dot_general(rows_of(grad_inner, jnp.int32(0), lax.ax...  274 us
    reduce_scatter x4, waiting for transfers between devices, local(): lax.psum_scatter(lax.dot_general(rows_of(active, jnp.int32(0), lax.axis_s...  268 us
    reduce_scatter x4, waiting for transfers between devices, local(): lax.psum_scatter(jnp.where(inside[:, None], picked.astype(jnp.float32), 0...  234 us
    dot_general x8, matrix products, head_rows_grad(): return jnp.dot(grad_logits, embedding, preferred_element_type=jnp.float32)  197 us
    all_gather x4, waiting for transfers between devices, local(): lax.all_gather(normed_two, 'mp', axis=0, tiled=True)  174 us
  transfers between devices with their start and end apart: 45, of which 40 were waited for; matrix products, arithmetic and copies ran while one was open for 18% of the time, Pallas kernels for 0%

commit v1 on v0

v1 whole, which is shorter than its diff:
```python
import functools

import jax
import jax.numpy as jnp
from jax import lax
from jax.experimental import pallas as pl
from jax.experimental.pallas import tpu as pltpu
from jax.sharding import PartitionSpec as P

HEAD_DIM = 64
EPS_NORM = 1e-05
ADAPTER_SCALE = 8.0
SCORE_SCALE = 0.125
MASK_VALUE = -1e30
CLIP_NORM = 1.0
BETA_ONE = 0.9
BETA_TWO = 0.999
LEARN_RATE = 0.01
WEIGHT_DECAY = 0.01
ADAM_EPS = 1e-08
HALO = 128
PAIR = 128
NT = (((1,), (1,)), ((), ()))
TN = (((0,), (0,)), ((), ()))
MESH = pl.DeviceIdType.MESH
VMEM_CAP = 62 * 2**20
LINE = 4
SIDE = 2


def is_own_mesh():
    return lax.axis_size("dp") == 4 and lax.axis_size("mp") == LINE * SIDE


def here():
    dp, mp = lax.axis_index("dp"), lax.axis_index("mp")
    return dp // 2, dp % 2, mp // SIDE, mp % SIDE


def dev(x, core, line, side):
    return {"dp": x * 2 + core, "mp": line * SIDE + side}


def greet(peers):
    barrier = pltpu.get_barrier_semaphore()
    for peer in peers:
        pl.semaphore_signal(barrier, inc=1, device_id=peer, device_id_type=MESH)
    pl.semaphore_wait(barrier, len(peers))


def greet_line(x, core, line, side, others):
    barrier = pltpu.get_barrier_semaphore()
    for peer in others:
        pl.semaphore_signal(barrier, inc=1, device_id=peer, device_id_type=MESH)

    @pl.when(line > 0)
    def _():
        pl.semaphore_signal(barrier, inc=1, device_id=dev(x, core, line - 1, side), device_id_type=MESH)

    @pl.when(line < LINE - 1)
    def _():
        pl.semaphore_signal(barrier, inc=1, device_id=dev(x, core, line + 1, side), device_id_type=MESH)

    inner = (line > 0) & (line < LINE - 1)

    @pl.when(inner)
    def _():
        pl.semaphore_wait(barrier, len(others) + 2)

    @pl.when(jnp.logical_not(inner))
    def _():
        pl.semaphore_wait(barrier, len(others) + 1)


def remote(src, dst, send_sem, recv_sem, peer):
    return pltpu.make_async_remote_copy(
        src_ref=src, dst_ref=dst, send_sem=send_sem, recv_sem=recv_sem, device_id=peer, device_id_type=MESH
    )


def swap_kernel(per_peer, src, dst, own_sem, send_sem, recv_sem):
    dp, mp = lax.axis_index("dp"), lax.axis_index("mp")
    count = LINE * SIDE
    peers = [{"dp": dp, "mp": lax.rem(mp + k, count)} for k in range(1, count)]
    greet(peers)
    copies = []
    for k in range(1, count):
        block = src.at[lax.rem(mp + k, count)] if per_peer else src
        copy = remote(block, dst.at[mp], send_sem.at[k], recv_sem.at[k], peers[k - 1])
        copy.start()
        copies.append(copy)
    own = pltpu.make_async_copy(src.at[mp] if per_peer else src, dst.at[mp], own_sem)
    own.start()
    own.wait()
    for copy in copies:
        copy.wait()


def swap(array, per_peer, collective):
    count = LINE * SIDE
    shape = array.shape if per_peer else (count,) + array.shape
    return pl.pallas_call(
        functools.partial(swap_kernel, per_peer),
        out_shape=jax.ShapeDtypeStruct(shape, array.dtype),
        in_specs=[pl.BlockSpec(memory_space=pltpu.VMEM)],
        out_specs=pl.BlockSpec(memory_space=pltpu.VMEM),
        scratch_shapes=[
            pltpu.SemaphoreType.DMA,
            pltpu.SemaphoreType.DMA((count,)),
            pltpu.SemaphoreType.DMA((count,)),
        ],
        compiler_params=pltpu.CompilerParams(
            collective_id=collective, has_side_effects=True, vmem_limit_bytes=VMEM_CAP
        ),
        name=f"swap_{collective}",
    )(array)


def agree_kernel(src, out, got, send_sem, recv_sem):
    dp, mp = lax.axis_index("dp"), lax.axis_index("mp")
    peers = [{"dp": lax.rem(dp + k, 4), "mp": mp} for k in range(1, 4)]
    greet(peers)
    copies = []
    for k in range(1, 4):
        copy = remote(src, got.at[k - 1], send_sem.at[k - 1], recv_sem.at[k - 1], peers[k - 1])
        copy.start()
        copies.append(copy)
    for copy in copies:
        copy.wait()
    out[...] = jnp.maximum(jnp.maximum(src[...], got[0]), jnp.maximum(got[1], got[2]))


def agree(values, collective):
    if not is_own_mesh():
        return lax.pmax(values, "dp")
    tile = jnp.zeros((8, 128), jnp.float32).at[0, : values.shape[0]].set(values)
    out = pl.pallas_call(
        agree_kernel,
        out_shape=jax.ShapeDtypeStruct((8, 128), jnp.float32),
        in_specs=[pl.BlockSpec(memory_space=pltpu.VMEM)],
        out_specs=pl.BlockSpec(memory_space=pltpu.VMEM),
        scratch_shapes=[
            pltpu.VMEM((3, 8, 128), jnp.float32),
            pltpu.SemaphoreType.DMA((3,)),
            pltpu.SemaphoreType.DMA((3,)),
        ],
        compiler_params=pltpu.CompilerParams(collective_id=collective, has_side_effects=True),
        name="agree",
    )(tile)
    return out[0, : values.shape[0]]


def weight_events(sizes):
    events, start = [], 0.0
    for k, size in enumerate(sizes):
        events.append((start - 1.5 * size - 0.001 if k else -1.0, "own", k, 0))
        for step in range(LINE):
            arrive = start + size * min(step, 2.5)
            if step:
                events.append((arrive, "line", k, step))
            events.append((arrive + 0.6 * size, "side", k, step))
            events.append((arrive + 1.2 * size, "x", k, step))
        start += 2.5 * size
    return sorted(events)


def weight_kernel(sizes, *refs):
    n = len(sizes)
    src, own_vmem, full = refs[:n], refs[n : 2 * n], refs[2 * n : 3 * n]
    own_sem = refs[3 * n]
    line_s, line_r, side_s, side_r, x_s, x_r, xf_s, xf_r, sib_s, sib_r, sib2_s, sib2_r, sib3_s, sib3_r = refs[3 * n + 1 :]
    x, core, line, side = here()
    up, down = dev(x, core, line + 1, side), dev(x, core, line - 1, side)
    across, twin, sibling = dev(x, core, line, 1 - side), dev(1 - x, core, line, side), dev(x, 1 - core, line, side)
    greet_line(x, core, line, side, [across, twin, sibling])
    mine = line * SIDE + side

    def piece(k, block, c, h):
        rows = full[k].shape[1]
        if h is None:
            return full[k].at[block, pl.ds(c * (rows // 2), rows // 2)]
        return full[k].at[block, pl.ds((c * 2 + h) * (rows // 4), rows // 4)]

    def own_piece(k, c, h):
        rows = full[k].shape[1]
        if h is None:
            return src[k].at[pl.ds(c * (rows // 2), rows // 2)]
        return src[k].at[pl.ds((c * 2 + h) * (rows // 4), rows // 4)]

    pending = []

    def when(cond, action):
        if cond is None:
            action()
        else:
            pl.when(cond)(action)

    def send(cond, src_ref, dst_ref, ssem, rsem, peer):
        copy = remote(src_ref, dst_ref, ssem, rsem, peer)
        when(cond, copy.start)
        pending.append((cond, copy))

    def arrived(cond, dst_ref, ssem, rsem):
        when(cond, remote(dst_ref, dst_ref, ssem, rsem, across).wait_recv)

    def exists(direction, step):
        if step == 0:
            return None
        return line >= step if direction == 0 else line + step < LINE

    def block_line(direction, step):
        return line - step if direction == 0 else line + step

    def flows(step):
        return (0,) if step == 0 else (0, 1)

    def both(first, second):
        return second if first is None else (first if second is None else first & second)

    def pass_on(k, step):
        for direction in flows(step):
            cond = exists(direction, step)
            block = block_line(direction, step) * SIDE + side
            far = step == LINE - 1
            whole = own_piece(k, core, None) if step == 0 else piece(k, block, core, None)
            part = own_piece(k, core, x) if step == 0 else piece(k, block, core, x)
            for way in (0, 1) if step == 0 else (direction,):
                if step < LINE - 1:
                    ok = both(cond, line < LINE - 1 if way == 0 else line > 0)
                    last = step + 1 == LINE - 1
                    send(
                        ok,
                        part if last else whole,
                        piece(k, block, core, x if last else None),
                        line_s.at[k, way, step],
                        line_r.at[k, way, step],
                        up if way == 0 else down,
                    )
            send(cond, part, piece(k, block, core, x), side_s.at[k, direction, step], side_r.at[k, direction, step], across)
            if far:
                send(cond, part, piece(k, block, core, x), xf_s.at[k, direction], xf_r.at[k, direction], twin)
            if step:
                send(
                    cond,
                    part if far else whole,
                    piece(k, block, core, x if far else None),
                    sib_s.at[k, direction, step],
                    sib_r.at[k, direction, step],
                    sibling,
                )

    for k in range(n):
        pltpu.make_async_copy(own_vmem[k], full[k].at[mine], own_sem.at[k]).start()

    for _, kind, k, step in weight_events(sizes):
        if kind == "own":
            pass_on(k, 0)
            continue
        for direction in flows(step):
            cond = exists(direction, step)
            near = block_line(direction, step) * SIDE + side
            other = block_line(direction, step) * SIDE + 1 - side
            far = step == LINE - 1
            if kind == "line":
                arrived(
                    cond,
                    piece(k, near, core, x if far else None),
                    line_s.at[k, direction, step - 1],
                    line_r.at[k, direction, step - 1],
                )
            elif kind == "side":
                part = piece(k, other, core, x)
                arrived(cond, part, side_s.at[k, direction, step], side_r.at[k, direction, step])
                send(cond, part, part, x_s.at[k, direction, step], x_r.at[k, direction, step], twin)
                send(cond, part, part, sib2_s.at[k, direction, step], sib2_r.at[k, direction, step], sibling)
            else:
                part = piece(k, other, core, 1 - x)
                arrived(cond, part, x_s.at[k, direction, step], x_r.at[k, direction, step])
                send(cond, part, part, sib3_s.at[k, direction, step], sib3_r.at[k, direction, step], sibling)
                if far:
                    part = piece(k, near, core, 1 - x)
                    arrived(cond, part, xf_s.at[k, direction], xf_r.at[k, direction])
                    send(cond, part, part, sib_s.at[k, direction, 0], sib_r.at[k, direction, 0], sibling)
        if kind == "line":
            pass_on(k, step)

    other_core = 1 - core
    for k in range(n):
        for step in range(LINE):
            for direction in flows(step):
                cond = exists(direction, step)
                near = block_line(direction, step) * SIDE + side
                other = block_line(direction, step) * SIDE + 1 - side
                far = step == LINE - 1
                if step:
                    arrived(
                        cond,
                        piece(k, near, other_core, x if far else None),
                        sib_s.at[k, direction, step],
                        sib_r.at[k, direction, step],
                    )
                if far:
                    arrived(cond, piece(k, near, other_core, 1 - x), sib_s.at[k, direction, 0], sib_r.at[k, direction, 0])
                arrived(cond, piece(k, other, other_core, x), sib2_s.at[k, direction, step], sib2_r.at[k, direction, step])
                arrived(cond, piece(k, other, other_core, 1 - x), sib3_s.at[k, direction, step], sib3_r.at[k, direction, step])
    for cond, copy in pending:
        when(cond, copy.wait_send)
    for k in range(n):
        pltpu.make_async_copy(own_vmem[k], full[k].at[mine], own_sem.at[k]).wait()


def gather_weights(blocks, collective):
    if not is_own_mesh():
        return [lax.all_gather(block, "mp", axis=0) for block in blocks]
    n = len(blocks)
    total = sum(block.size for block in blocks)
    sizes = [block.size / total for block in blocks]
    grid = pltpu.SemaphoreType.DMA((n, 2, LINE))
    pair = pltpu.SemaphoreType.DMA((n, 2))
    return pl.pallas_call(
        functools.partial(weight_kernel, sizes),
        out_shape=[jax.ShapeDtypeStruct((LINE * SIDE,) + block.shape, block.dtype) for block in blocks],
        in_specs=[pl.BlockSpec(memory_space=pl.ANY)] * n + [pl.BlockSpec(memory_space=pltpu.VMEM)] * n,
        out_specs=[pl.BlockSpec(memory_space=pl.ANY)] * n,
        scratch_shapes=[pltpu.SemaphoreType.DMA((n,)), grid, grid, grid, grid, grid, grid, pair, pair]
        + [grid] * 6,
        compiler_params=pltpu.CompilerParams(
            collective_id=collective, has_side_effects=True, vmem_limit_bytes=VMEM_CAP
        ),
        name="gather_weights",
    )(*blocks, *blocks)


def spread_kernel(own, out, own_sem, line_s, line_r, side_s, side_r):
    x, core, line, side = here()
    across = dev(x, core, line, 1 - side)
    greet_line(x, core, line, side, [across])
    up, down = dev(x, core, line + 1, side), dev(x, core, line - 1, side)
    mine = line * SIDE + side
    local = pltpu.make_async_copy(own, out.at[mine], own_sem)
    local.start()
    pending = []

    def send(cond, src, block, ssem, rsem, peer):
        copy = remote(src, out.at[block], ssem, rsem, peer)
        if cond is None:
            copy.start()
        else:
            pl.when(cond)(copy.start)
        pending.append((cond, copy))

    send(line < LINE - 1, own, mine, line_s.at[0, 0], line_r.at[0, 0], up)
    send(line > 0, own, mine, line_s.at[1, 0], line_r.at[1, 0], down)
    send(None, own, mine, side_s.at[0, 0], side_r.at[0, 0], across)
    for step in range(1, LINE):
        for way in (0, 1):
            cond = line >= step if way == 0 else line + step < LINE
            block = (line - step if way == 0 else line + step) * SIDE + side
            pl.when(cond)(
                remote(out.at[block], out.at[block], line_s.at[way, step - 1], line_r.at[way, step - 1], across).wait_recv
            )
            if step < LINE - 1:
                more = cond & (line < LINE - 1 if way == 0 else line > 0)
                send(more, out.at[block], block, line_s.at[way, step], line_r.at[way, step], up if way == 0 else down)
            send(cond, out.at[block], block, side_s.at[way, step], side_r.at[way, step], across)
    for step in range(LINE):
        for way in (0,) if step == 0 else (0, 1):
            cond = line >= step if way == 0 else line + step < LINE
            block = (line - step if way == 0 else line + step) * SIDE + 1 - side
            pl.when(cond)(
                remote(out.at[block], out.at[block], side_s.at[way, step], side_r.at[way, step], across).wait_recv
            )
    for cond, copy in pending:
        if cond is None:
            copy.wait_send()
        else:
            pl.when(cond)(copy.wait_send)
    local.wait()


def spread(rows, collective):
    if not is_own_mesh():
        return lax.all_gather(rows, "mp", axis=0)
    sems = pltpu.SemaphoreType.DMA((2, LINE))
    return pl.pallas_call(
        spread_kernel,
        out_shape=jax.ShapeDtypeStruct((LINE * SIDE,) + rows.shape, rows.dtype),
        in_specs=[pl.BlockSpec(memory_space=pltpu.VMEM)],
        out_specs=pl.BlockSpec(memory_space=pl.ANY),
        scratch_shapes=[pltpu.SemaphoreType.DMA, sems, sems, sems, sems],
        compiler_params=pltpu.CompilerParams(
            collective_id=collective, has_side_effects=True, vmem_limit_bytes=VMEM_CAP
        ),
        name=f"spread_{collective}",
    )(rows)


def collect_order(line, step):
    mirror = line // 2
    near = line * (1 - mirror) + (LINE - 1 - line) * mirror
    place = (LINE - 1, LINE - 2, 1 - near, near)[step]
    return place * (1 - mirror) + (LINE - 1 - place) * mirror


def collect_kernel(src, out, side_got, line_out, line_got, side_s, side_r, line_s, line_r):
    x, core, line, side = here()
    across = dev(x, core, line, 1 - side)
    greet_line(x, core, line, side, [across])
    up, down = dev(x, core, line + 1, side), dev(x, core, line - 1, side)
    copies = []
    for step in range(LINE):
        dest = collect_order(line, step)
        copy = remote(
            src.at[dest * SIDE + 1 - side], side_got.at[step], side_s.at[step], side_r.at[step], across
        )
        copy.start()
        copies.append(copy)

    def add(target, more):
        target[...] = (target[...].astype(jnp.float32) + more[...].astype(jnp.float32)).astype(target.dtype)

    for step in range(LINE):
        dest = collect_order(line, step)
        copies[step].wait_recv()
        partial = line_out.at[step]
        partial[...] = (
            src[dest * SIDE + side].astype(jnp.float32) + side_got[step].astype(jnp.float32)
        ).astype(partial.dtype)
        for way in (0, 1):
            behind = line > 0 if way == 0 else line < LINE - 1
            onward = dest >= line if way == 0 else dest <= line

            @pl.when(behind & onward)
            def _():
                got = line_got.at[way, dest]
                remote(got, got, line_s.at[way, step], line_r.at[way, dest], across).wait_recv()
                add(partial, got)

        for way in (0, 1):
            onward = dest > line if way == 0 else dest < line

            @pl.when(onward)
            def _():
                remote(
                    partial, line_got.at[way, dest], line_s.at[way, step], line_r.at[way, dest], up if way == 0 else down
                ).start()

    out[...] = line_out[LINE - 1]
    for step in range(LINE):
        dest = collect_order(line, step)
        copies[step].wait_send()
        for way in (0, 1):

            @pl.when(dest > line if way == 0 else dest < line)
            def _():
                remote(
                    line_out.at[step], line_got.at[way, dest], line_s.at[way, step], line_r.at[way, dest], across
                ).wait_send()


def collect(parts, collective):
    if not is_own_mesh():
        return lax.psum_scatter(parts, "mp", scatter_dimension=0)
    shape = parts.shape[1:]
    sems = pltpu.SemaphoreType.DMA((LINE,))
    pairs = pltpu.SemaphoreType.DMA((2, LINE))
    return pl.pallas_call(
        collect_kernel,
        out_shape=jax.ShapeDtypeStruct(shape, parts.dtype),
        in_specs=[pl.BlockSpec(memory_space=pltpu.VMEM)],
        out_specs=pl.BlockSpec(memory_space=pltpu.VMEM),
        scratch_shapes=[
            pltpu.VMEM((LINE,) + shape, parts.dtype),
            pltpu.VMEM((LINE,) + shape, parts.dtype),
            pltpu.VMEM((2, LINE) + shape, parts.dtype),
            sems,
            sems,
            pairs,
            pairs,
        ],
        compiler_params=pltpu.CompilerParams(
            collective_id=collective, has_side_effects=True, vmem_limit_bytes=VMEM_CAP
        ),
        name=f"collect_{collective}",
    )(parts)


def head_kernel(tile, tiles, x_ref, target_ref, table_ref, grad_ref, total_ref, logit_scr, acc):
    rows = x_ref.shape[0]
    target = target_ref[...]

    def table_rows(t):
        return table_ref[pl.ds(pl.multiple_of(t * tile, tile), tile), :]

    def logits(t):
        return lax.dot_general(x_ref[...], table_rows(t), NT, preferred_element_type=jnp.float32)

    logit_scr[0] = logits(0)
    acc[...] = jnp.zeros_like(acc)

    def lap(t, carry):
        peak, total = carry
        slot = t % 2

        @pl.when(t + 1 < tiles)
        def _():
            logit_scr[1 - slot] = logits(t + 1)

        scores = logit_scr[slot]
        new_peak = jnp.maximum(peak, jnp.max(scores, axis=-1, keepdims=True))
        prob = jnp.exp(scores - new_peak)
        shrink = jnp.exp(peak - new_peak)
        total = total * shrink + jnp.sum(prob, axis=-1, keepdims=True)
        column = lax.broadcasted_iota(jnp.int32, scores.shape, 1) + t * tile
        others = jnp.where(column == target, 0.0, prob).astype(jnp.bfloat16)
        acc[...] = acc[...] * shrink + jnp.dot(others, table_rows(t), preferred_element_type=jnp.float32)
        return new_peak, total

    start = (jnp.full((rows, 1), MASK_VALUE, jnp.float32), jnp.zeros((rows, 1), jnp.float32))
    peak, total = lax.fori_loop(0, tiles, lap, start)
    grad_ref[...] = acc[...] / total
    total_ref[...] = jnp.broadcast_to(peak + jnp.log(total), total_ref.shape)


def largest_block(extent, choices):
    for choice in choices:
        if extent % choice == 0:
            return choice
    return extent


def head(rows_in, target, table):
    count, width = rows_in.shape
    vocab = table.shape[0]
    tile = largest_block(vocab, (1280, 640, 256, 128))
    rows = largest_block(count, (384, 512, 256, 128))
    return pl.pallas_call(
        functools.partial(head_kernel, tile, vocab // tile),
        out_shape=(
            jax.ShapeDtypeStruct((count, width), jnp.float32),
            jax.ShapeDtypeStruct((count, 128), jnp.float32),
        ),
        grid=(count // rows,),
        in_specs=[
            pl.BlockSpec((rows, width), lambda i: (i, 0)),
            pl.BlockSpec((rows, 1), lambda i: (i, 0)),
            pl.BlockSpec((vocab, width), lambda i: (0, 0), pipeline_mode=pl.Buffered(1)),
        ],
        out_specs=(
            pl.BlockSpec((rows, width), lambda i: (i, 0)),
            pl.BlockSpec((rows, 128), lambda i: (i, 0)),
        ),
        scratch_shapes=[pltpu.VMEM((2, rows, tile), jnp.float32), pltpu.VMEM((rows, width), jnp.float32)],
        compiler_params=pltpu.CompilerParams(vmem_limit_bytes=VMEM_CAP),
        name=f"head_{count}",
    )(rows_in, target, table)


def norm_parts(values):
    center = values - jnp.mean(values, axis=-1, keepdims=True)
    spread_of = jnp.mean(center * center, axis=-1, keepdims=True)
    scale = lax.rsqrt(spread_of + EPS_NORM)
    return center * scale, scale


def layer_norm(values, gain_row):
    return norm_parts(values)[0] * gain_row


def norm_back(values, gain_row, grad_out):
    hat, scale = norm_parts(values)
    inner = grad_out * gain_row
    return scale * (
        inner
        - jnp.mean(inner, axis=-1, keepdims=True)
        - hat * jnp.mean(inner * hat, axis=-1, keepdims=True)
    )


GELU_A = 0.7978845608028654
GELU_B = 0.044715


def gelu(z):
    return 0.5 * z * (1.0 + jnp.tanh(GELU_A * (z + GELU_B * z * z * z)))


def gelu_slope(z):
    square = z * z
    curve = jnp.tanh(GELU_A * z * (1.0 + GELU_B * square))
    return 0.5 * (1.0 + curve) + 0.5 * z * (1.0 - curve * curve) * GELU_A * (1.0 + 3.0 * GELU_B * square)


def row_blocks(count, body, block=128):
    def lap(i, carry):
        body(pl.ds(pl.multiple_of(i * block, block), block))
        return carry

    lax.fori_loop(0, count // block, lap, 0)


def allowed_keys(seg_col, seg_row, block):
    rows = seg_col[HALO + block * PAIR : HALO + (block + 1) * PAIR, :]
    keys = seg_row[:, block * PAIR : block * PAIR + 2 * PAIR]
    shape = (PAIR, 2 * PAIR)
    causal = lax.broadcasted_iota(jnp.int32, shape, 1) <= lax.broadcasted_iota(jnp.int32, shape, 0) + HALO
    return causal & (rows == keys)


def head_lanes(shape, which):
    lane = lax.broadcasted_iota(jnp.int32, shape, 1)
    return lane < HEAD_DIM if which == 0 else lane >= HEAD_DIM


def only_head(values, which):
    return jnp.where(head_lanes(values.shape, which), values, jnp.zeros_like(values))


def probs_of(query, keys, which, allowed):
    scores = lax.dot_general(only_head(query, which), keys, NT, preferred_element_type=jnp.float32) * SCORE_SCALE
    scores = jnp.where(allowed, scores, MASK_VALUE)
    exp_blk = jnp.exp(scores - jnp.max(scores, axis=-1, keepdims=True))
    return exp_blk / jnp.sum(exp_blk, axis=-1, keepdims=True)


def forward_kernel(
    emb,
    pos,
    seg_col,
    seg_row,
    rank_row,
    gains,
    down,
    up_query,
    up_value,
    wq_hbm,
    wo_hbm,
    w1_hbm,
    w2_hbm,
    rows_out,
    pick_out,
    normed_out,
    low_out,
    query_out,
    key_out,
    value_out,
    one_out,
    two_out,
    fc_out,
    wq,
    wo,
    w1,
    w2,
    wide,
    attn,
    normed_two,
    fc_buf,
    wq_sem,
    w_sem,
    fc_sem,
):
    tokens = two_out.shape[0]
    reach = HALO + tokens
    pairs = query_out.shape[0]
    chunks = w1.shape[0]
    loads = []
    for p in range(pairs):
        loads.append(
            pltpu.make_async_copy(
                wq_hbm.at[p, pl.ds(0, wq.shape[1])], wq.at[p // 2, :, pl.ds((p % 2) * 3 * PAIR, 3 * PAIR)], wq_sem.at[p]
            )
        )
    others = [
        pltpu.make_async_copy(a, b, w_sem.at[i]) for i, (a, b) in enumerate(((wo_hbm, wo), (w1_hbm, w1), (w2_hbm, w2)))
    ]
    for load in loads + others:
        load.start()

    def first(rows):
        x_zero = emb[rows, :].astype(jnp.float32) + pos[rows, :].astype(jnp.float32)
        wide[rows, :] = x_zero
        normed_out[rows, :] = layer_norm(x_zero, gains[0:1, :]).astype(jnp.bfloat16)

    row_blocks(reach, first)
    low_out[...] = lax.dot_general(normed_out[...], down[...], NT, preferred_element_type=jnp.float32).astype(
        jnp.bfloat16
    )
    for load in loads:
        load.wait()

    def project(j, carry):
        both = jnp.dot(normed_out[...], wq[j], preferred_element_type=jnp.float32)
        for half in range(2):
            p = 2 * j + half
            cols = pl.ds(pl.multiple_of(p * PAIR, PAIR), PAIR)
            base = half * 3 * PAIR
            term_q = jnp.dot(low_out[HALO:, :], up_query[:, cols], preferred_element_type=jnp.float32)
            term_v = jnp.dot(low_out[...], up_value[:, cols], preferred_element_type=jnp.float32)
            query_out[p] = (both[HALO:, base : base + PAIR] + term_q).astype(jnp.bfloat16)
            key_out[p] = both[:, base + PAIR : base + 2 * PAIR].astype(jnp.bfloat16)
            value_out[p] = (both[:, base + 2 * PAIR : base + 3 * PAIR] + term_v).astype(jnp.bfloat16)
        return carry

    lax.fori_loop(0, pairs // 2, project, 0)

    def attend(p, carry):
        cols = pl.ds(pl.multiple_of(p * PAIR, PAIR), PAIR)
        for block in range(tokens // PAIR):
            allowed = allowed_keys(seg_col, seg_row, block)
            rows = slice(block * PAIR, (block + 1) * PAIR)
            window = slice(block * PAIR, block * PAIR + 2 * PAIR)
            query, keys, values = query_out[p, rows, :], key_out[p, window, :], value_out[p, window, :]
            mixed = [
                jnp.dot(probs_of(query, keys, h, allowed).astype(jnp.bfloat16), values, preferred_element_type=jnp.float32)
                for h in range(2)
            ]
            attn[rows, cols] = jnp.where(head_lanes(mixed[0].shape, 0), mixed[0], mixed[1]).astype(jnp.bfloat16)
        return carry

    lax.fori_loop(0, pairs, attend, 0)
    others[0].wait()
    one_out[...] = wide[HALO:, :] + jnp.dot(attn[...], wo[...], preferred_element_type=jnp.float32)

    def second(rows):
        normed_two[rows, :] = layer_norm(one_out[rows, :], gains[1:2, :]).astype(jnp.bfloat16)
        two_out[rows, :] = one_out[rows, :]

    row_blocks(tokens, second)
    others[1].wait()
    others[2].wait()

    def save(c):
        return pltpu.make_async_copy(fc_buf.at[c % 2], fc_out.at[c], fc_sem.at[c % 2])

    def feed(c, carry):
        @pl.when(c >= 2)
        def _():
            save(c - 2).wait()

        inner = jnp.dot(normed_two[...], w1[c], preferred_element_type=jnp.float32)
        fc_buf[c % 2] = inner
        save(c).start()
        two_out[...] += lax.dot_general(
            gelu(inner).astype(jnp.bfloat16), w2[c], NT, preferred_element_type=jnp.float32
        )
        return carry

    lax.fori_loop(0, chunks, feed, 0)
    save(chunks - 2).wait()
    save(chunks - 1).wait()

    def third(rows):
        final = layer_norm(two_out[rows, :], gains[2:3, :]).astype(jnp.bfloat16)
        attn[rows, :] = final
        later = pl.ds(rows.start + reach, rows.size)
        picked = jnp.sum(final.astype(jnp.float32) * emb[later, :].astype(jnp.float32), axis=-1, keepdims=True)
        pick_out[rows, :] = jnp.broadcast_to(picked, (rows.size, pick_out.shape[1]))

    row_blocks(tokens, third)
    place = lax.broadcasted_iota(jnp.int32, (tokens, tokens), 0)
    rows_out[...] = jnp.dot(
        (place == rank_row[...]).astype(jnp.bfloat16), attn[...], preferred_element_type=jnp.float32
    ).astype(jnp.bfloat16)


def forward(emb, pos, seg_col, seg_row, rank_row, gains, down, up_query, up_value, weights):
    wq, wo, w1, w2 = weights
    reach, width = pos.shape
    tokens = reach - HALO
    pairs, chunks, hidden = wq.shape[0], w1.shape[0], w1.shape[2]
    f32, bf16 = jnp.float32, jnp.bfloat16
    vmem, hbm = pl.BlockSpec(memory_space=pltpu.VMEM), pl.BlockSpec(memory_space=pl.ANY)
    return pl.pallas_call(
        forward_kernel,
        out_shape=(
            jax.ShapeDtypeStruct((tokens, width), bf16),
            jax.ShapeDtypeStruct((tokens, 128), f32),
            jax.ShapeDtypeStruct((reach, width), bf16),
            jax.ShapeDtypeStruct((reach, 128), bf16),
            jax.ShapeDtypeStruct((pairs, tokens, PAIR), bf16),
            jax.ShapeDtypeStruct((pairs, reach, PAIR), bf16),
            jax.ShapeDtypeStruct((pairs, reach, PAIR), bf16),
            jax.ShapeDtypeStruct((tokens, width), f32),
            jax.ShapeDtypeStruct((tokens, width), f32),
            jax.ShapeDtypeStruct((chunks, tokens, hidden), f32),
        ),
        in_specs=[vmem] * 9 + [hbm] * 4,
        out_specs=(vmem,) * 9 + (hbm,),
        scratch_shapes=[
            pltpu.VMEM((pairs // 2, width, 6 * PAIR), bf16),
            pltpu.VMEM(wo.shape, bf16),
            pltpu.VMEM(w1.shape, bf16),
            pltpu.VMEM(w2.shape, bf16),
            pltpu.VMEM((reach, width), f32),
            pltpu.VMEM((tokens, width), bf16),
            pltpu.VMEM((tokens, width), bf16),
            pltpu.VMEM((2, tokens, hidden), f32),
            pltpu.SemaphoreType.DMA((pairs,)),
            pltpu.SemaphoreType.DMA((3,)),
            pltpu.SemaphoreType.DMA((2,)),
        ],
        compiler_params=pltpu.CompilerParams(vmem_limit_bytes=VMEM_CAP),
        name="forward",
    )(emb, pos, seg_col, seg_row, rank_row, gains, down, up_query, up_value, wq, wo, w1, w2)


def backward_kernel(
    grad_rows,
    lse_row,
    rank_col,
    pick,
    weight_col,
    target_emb,
    one,
    two,
    gains,
    seg_col,
    seg_row,
    query,
    key,
    value,
    normed,
    low,
    up_query,
    up_value,
    fc_hbm,
    wo_hbm,
    w1_hbm,
    w2_hbm,
    out,
    wo,
    w1,
    w2,
    fc_buf,
    grad_two,
    grad_low,
    grad_inner,
    grad_mixed,
    grad_query,
    grad_value,
    w_sem,
    fc_sem,
):
    tokens, width = two.shape
    pairs, chunks = query.shape[0], w1.shape[0]
    loads = [
        pltpu.make_async_copy(a, b, w_sem.at[i]) for i, (a, b) in enumerate(((w2_hbm, w2), (w1_hbm, w1), (wo_hbm, wo)))
    ]

    def fetch(c):
        return pltpu.make_async_copy(fc_hbm.at[c], fc_buf.at[c % 2], fc_sem.at[c % 2])

    loads[0].start()
    fetch(0).start()
    loads[1].start()
    loads[2].start()

    chosen = rank_col[...] == lax.broadcasted_iota(jnp.int32, (tokens, tokens), 1)
    grad_two[...] = jnp.dot(chosen.astype(jnp.bfloat16), grad_rows[...], preferred_element_type=jnp.float32)
    lse = jnp.sum(jnp.where(chosen, lse_row[...], 0.0), axis=-1, keepdims=True)
    weight = weight_col[...]
    loss = jnp.sum(weight * (lse - pick[:, 0:1]))
    grad_value[0:tokens, 0:128] = jnp.broadcast_to(jnp.exp(pick[:, 0:1] - lse) - 1.0, (tokens, 128))

    def first(rows):
        factor = grad_value[rows, 0:1]
        grad_final = weight_col[rows, :] * (grad_two[rows, :] + factor * target_emb[rows, :].astype(jnp.float32))
        grad = norm_back(two[rows, :], gains[2:3, :], grad_final)
        grad_two[rows, :] = grad
        grad_low[rows, :] = grad.astype(jnp.bfloat16)

    row_blocks(tokens, first)
    grad_inner[...] = jnp.zeros_like(grad_inner)
    for load in loads[:2]:
        load.wait()

    def feed(c, carry):
        fetch(c).wait()

        @pl.when(c + 1 < chunks)
        def _():
            fetch(c + 1).start()

        grad_act = jnp.dot(grad_low[...], w2[c], preferred_element_type=jnp.float32)
        grad_in = (grad_act * gelu_slope(fc_buf[c % 2])).astype(jnp.bfloat16)
        grad_inner[...] += lax.dot_general(grad_in, w1[c], NT, preferred_element_type=jnp.float32)
        return carry

    lax.fori_loop(0, chunks, feed, 0)

    def second(rows):
        grad_one = grad_two[rows, :] + norm_back(one[rows, :], gains[1:2, :], grad_inner[rows, :])
        grad_low[rows, :] = grad_one.astype(jnp.bfloat16)

    row_blocks(tokens, second)
    loads[2].wait()
    grad_mixed[...] = lax.dot_general(grad_low[...], wo[...], NT, preferred_element_type=jnp.float32).astype(jnp.bfloat16)
    grad_value[...] = jnp.zeros_like(grad_value)

    def attend(p, carry):
        cols = pl.ds(pl.multiple_of(p * PAIR, PAIR), PAIR)
        for block in range(tokens // PAIR):
            allowed = allowed_keys(seg_col, seg_row, block)
            rows = slice(block * PAIR, (block + 1) * PAIR)
            window = slice(block * PAIR, block * PAIR + 2 * PAIR)
            keys, values, mixed = key[p, window, :], value[p, window, :], grad_mixed[rows, cols]
            grads_q, grads_v = [], []
            for h in range(2):
                prob = probs_of(query[p, rows, :], keys, h, allowed)
                grad_prob = lax.dot_general(only_head(mixed, h), values, NT, preferred_element_type=jnp.float32)
                inner = jnp.sum(prob * grad_prob, axis=-1, keepdims=True)
                grad_score = (prob * (grad_prob - inner)).astype(jnp.bfloat16)
                grads_q.append(jnp.dot(grad_score, keys, preferred_element_type=jnp.float32) * SCORE_SCALE)
                grads_v.append(lax.dot_general(prob.astype(jnp.bfloat16), mixed, TN, preferred_element_type=jnp.float32))
            grad_query[rows, cols] = jnp.where(head_lanes(grads_q[0].shape, 0), grads_q[0], grads_q[1]).astype(
                jnp.bfloat16
            )
            grad_value[window, cols] += jnp.where(head_lanes(grads_v[0].shape, 0), grads_v[0], grads_v[1])
        return carry

    lax.fori_loop(0, pairs, attend, 0)
    grad_v = grad_value[...].astype(jnp.bfloat16)
    grad_q = grad_query[...]
    low_q = lax.dot_general(grad_q, up_query[...], NT, preferred_element_type=jnp.float32).astype(jnp.bfloat16)
    low_v = lax.dot_general(grad_v, up_value[...], NT, preferred_element_type=jnp.float32).astype(jnp.bfloat16)
    grad_down = lax.dot_general(low_q, normed[HALO:, :], TN, preferred_element_type=jnp.float32)
    grad_down += lax.dot_general(low_v, normed[...], TN, preferred_element_type=jnp.float32)
    up_q = lax.dot_general(low[HALO:, :], grad_q, TN, preferred_element_type=jnp.float32)
    up_v = lax.dot_general(low[...], grad_v, TN, preferred_element_type=jnp.float32)
    out[0:8, :] = grad_down[0:8, :]
    first_rows = lax.broadcasted_iota(jnp.int32, (8, width), 0) < 4
    out[8:16, :] = ADAPTER_SCALE * jnp.where(first_rows, up_q[0:8, :], up_v[0:8, :])
    out[16:24, :] = jnp.broadcast_to(loss, (8, width))


def backward(grad_rows, lse_row, rank_col, pick, weight_col, target_emb, saved, gains, seg_col, seg_row, up_query, up_value, weights):
    normed, low, query, key, value, one, two, fc = saved
    _, wo, w1, w2 = weights
    tokens, width = one.shape
    reach, hidden = normed.shape[0], w1.shape[2]
    f32, bf16 = jnp.float32, jnp.bfloat16
    vmem, hbm = pl.BlockSpec(memory_space=pltpu.VMEM), pl.BlockSpec(memory_space=pl.ANY)
    return pl.pallas_call(
        backward_kernel,
        out_shape=jax.ShapeDtypeStruct((24, width), f32),
        in_specs=[vmem] * 18 + [hbm] * 4,
        out_specs=vmem,
        scratch_shapes=[
            pltpu.VMEM(wo.shape, bf16),
            pltpu.VMEM(w1.shape, bf16),
            pltpu.VMEM(w2.shape, bf16),
            pltpu.VMEM((2, tokens, hidden), f32),
            pltpu.VMEM((tokens, width), f32),
            pltpu.VMEM((tokens, width), bf16),
            pltpu.VMEM((tokens, width), f32),
            pltpu.VMEM((tokens, width), bf16),
            pltpu.VMEM((tokens, width), bf16),
            pltpu.VMEM((reach, width), f32),
            pltpu.SemaphoreType.DMA((3,)),
            pltpu.SemaphoreType.DMA((2,)),
        ],
        compiler_params=pltpu.CompilerParams(vmem_limit_bytes=VMEM_CAP),
        name="backward",
    )(
        grad_rows, lse_row, rank_col, pick, weight_col, target_emb, one, two, gains, seg_col, seg_row,
        query, key, value, normed, low, up_query, up_value, fc, wo, w1, w2,
    )


def finish_kernel(
    src, master, first, second, mask, scalars, stats, new_first, new_second, new_master, new_copy,
    got, squares, squares_got, own_sem, send_sem, recv_sem, send_two, recv_two,
):
    dp, mp = lax.axis_index("dp"), lax.axis_index("mp")
    groups, copies_of = LINE * SIDE, 4
    total = groups * copies_of
    peers = [
        {"dp": lax.rem(dp + k // groups, copies_of), "mp": lax.rem(mp + k % groups, groups)} for k in range(1, total)
    ]
    greet(peers)
    copies = []
    for k in range(1, total):
        copy = remote(
            src.at[lax.rem(mp + k % groups, groups)], got.at[k], send_sem.at[k], recv_sem.at[k], peers[k - 1]
        )
        copy.start()
        copies.append(copy)
    own = pltpu.make_async_copy(src.at[mp], got.at[0], own_sem)
    own.start()
    own.wait()
    grads = got[0]
    for k in range(1, total):
        copies[k - 1].wait_recv()
    for k in range(1, total):
        grads = grads + got[k]
    loss = grads[16:24, :]
    grads = grads[0:16, :]
    squares[...] = jnp.broadcast_to(jnp.sum(grads * grads), squares.shape)
    again = []
    for k in range(1, groups):
        copy = remote(squares, squares_got.at[k], send_two.at[k], recv_two.at[k], peers[k - 1])
        copy.start()
        again.append(copy)
    for copy in again:
        copy.wait()
    square_sum = squares[...]
    for k in range(1, groups):
        square_sum = square_sum + squares_got[k]
    norm = jnp.sqrt(square_sum)
    stats[0] = loss
    stats[1] = norm
    clipped = grads * jnp.minimum(1.0, CLIP_NORM / (norm[0:1, :] + 1e-06))
    one = BETA_ONE * first[...] + (1.0 - BETA_ONE) * clipped
    two = BETA_TWO * second[...] + (1.0 - BETA_TWO) * clipped * clipped
    one_hat = one / scalars[0:1, :]
    two_hat = two / scalars[1:2, :]
    weight = master[...] - LEARN_RATE * (one_hat / (jnp.sqrt(two_hat) + ADAM_EPS) + WEIGHT_DECAY * master[...])
    keep = mask[...]
    new_first[...] = keep * one
    new_second[...] = keep * two
    new_master[...] = keep * weight
    new_copy[...] = (keep * weight).astype(jnp.bfloat16)
    for copy in copies:
        copy.wait_send()


def finish(grads, master, first, second, mask, scalars, collective):
    groups = lax.axis_size("mp")
    width = grads.shape[1]
    cols = width // groups
    slices = jnp.transpose(grads.reshape(24, groups, cols), (1, 0, 2))
    if not is_own_mesh():
        summed = lax.psum(lax.psum_scatter(slices, "mp", scatter_dimension=0), "dp")
        owned = summed[:16]
        norm = jnp.sqrt(lax.psum(jnp.sum(owned * owned), "mp"))
        clipped = owned * jnp.minimum(1.0, CLIP_NORM / (norm + 1e-06))
        one = BETA_ONE * first + (1.0 - BETA_ONE) * clipped
        two = BETA_TWO * second + (1.0 - BETA_TWO) * clipped * clipped
        weight = master - LEARN_RATE * (
            one / scalars[0, 0] / (jnp.sqrt(two / scalars[1, 0]) + ADAM_EPS) + WEIGHT_DECAY * master
        )
        kept = mask * weight
        return summed[16, 0], norm, mask * one, mask * two, kept, kept.astype(jnp.bfloat16)
    vmem = pl.BlockSpec(memory_space=pltpu.VMEM)
    tile = jax.ShapeDtypeStruct((16, cols), jnp.float32)
    total = groups * 4
    stats, one, two, weight, copy = pl.pallas_call(
        finish_kernel,
        out_shape=(jax.ShapeDtypeStruct((2, 8, cols), jnp.float32), tile, tile, tile, jax.ShapeDtypeStruct((16, cols), jnp.bfloat16)),
        in_specs=[vmem] * 6,
        out_specs=(vmem,) * 5,
        scratch_shapes=[
            pltpu.VMEM((total, 24, cols), jnp.float32),
            pltpu.VMEM((8, cols), jnp.float32),
            pltpu.VMEM((groups, 8, cols), jnp.float32),
            pltpu.SemaphoreType.DMA,
            pltpu.SemaphoreType.DMA((total,)),
            pltpu.SemaphoreType.DMA((total,)),
            pltpu.SemaphoreType.DMA((groups,)),
            pltpu.SemaphoreType.DMA((groups,)),
        ],
        compiler_params=pltpu.CompilerParams(collective_id=collective, has_side_effects=True),
        name="finish",
    )(slices, master, first, second, mask, scalars)
    return stats[0, 0, 0], stats[1, 0, 0], one, two, weight, copy


ROUND_ROWS = 80


def fetch_rows(embedding, ids, parts, tokens, collective):
    groups, mine = lax.axis_size("mp"), lax.axis_index("mp")
    vocab_local, width = embedding.shape
    seq = ids.shape[1]
    reach = HALO + tokens
    window = reach + 8
    spots = jnp.arange(parts)[:, None] * tokens - HALO + jnp.arange(window)[None, :]
    spots = jnp.clip(spots, 0, seq - 1)
    wanted = ids[:, spots].reshape(groups, window)
    holder = wanted // vocab_local
    if not is_own_mesh():
        near = wanted - mine * vocab_local
        inside = (near >= 0) & (near < vocab_local)
        rows = jnp.where(inside[..., None], jnp.take(embedding, jnp.clip(near, 0, vocab_local - 1), axis=0), 0)
        rows = lax.psum_scatter(rows, "mp", scatter_dimension=0)
        rows = jnp.concatenate([rows[:reach], rows[HALO + 1 : HALO + 1 + tokens]], axis=0)
        return jnp.float32(0.0), lambda rounds: rows
    earlier = jnp.arange(window)[:, None] > jnp.arange(window)[None, :]
    same = wanted[:, :, None] == wanted[:, None, :]
    lead = jnp.logical_not(jnp.any(same & earlier[None], axis=2))
    below = (holder[:, :, None] == holder[:, None, :]) & (wanted[:, None, :] < wanted[:, :, None]) & lead[:, None, :]
    slot = jnp.sum(below.astype(jnp.int32), axis=2)
    need = (jnp.max(slot) + 1).astype(jnp.float32)
    asked = lead & (holder == mine)
    my_slot = lax.dynamic_index_in_dim(slot, mine, 0, keepdims=False)
    my_holder = lax.dynamic_index_in_dim(holder, mine, 0, keepdims=False)

    def listed(values):
        return jnp.concatenate([values[:reach], values[HALO + 1 : HALO + 1 + tokens]])

    list_slot, list_holder = listed(my_slot), listed(my_holder)

    def one_round(r):
        base = r * ROUND_ROWS
        hit = asked[:, None, :] & (slot[:, None, :] == base + jnp.arange(ROUND_ROWS)[None, :, None])
        chosen = jnp.sum(jnp.where(hit, wanted[:, None, :] - mine * vocab_local, 0), axis=2)
        rows = jnp.take(embedding, chosen.reshape(-1), axis=0, mode="clip").reshape(groups, ROUND_ROWS, width)
        got = swap(rows, True, collective).reshape(groups * ROUND_ROWS, width)
        place = list_slot - base
        place = jnp.where((place >= 0) & (place < ROUND_ROWS), list_holder * ROUND_ROWS + place, -1)
        pick = (place[:, None] == jnp.arange(groups * ROUND_ROWS)[None, :]).astype(jnp.bfloat16)
        return jnp.dot(pick, got, preferred_element_type=jnp.float32).astype(jnp.bfloat16)

    def all_rounds(rounds):
        def lap(state):
            r, so_far = state
            return r + 1, so_far + one_round(r)

        return lax.while_loop(lambda state: state[0] < rounds, lap, (jnp.int32(1), one_round(jnp.int32(0))))[1]

    return need, all_rounds


def local(
    packed_token_rows,
    example_numbers,
    completion,
    global_token_count,
    owners,
    optimizer_step,
    embedding,
    positions,
    gains,
    query_key_value_weight,
    attention_output_weight,
    feedforward_input_weight,
    feedforward_output_weight,
    adapter_down_weight,
    adapter_up_weight,
    master,
    first_moment,
    second_moment,
):
    groups, mine = lax.axis_size("mp"), lax.axis_index("mp")
    batch, seq = packed_token_rows.shape
    width = embedding.shape[1]
    vocab_local = embedding.shape[0]
    tokens = batch * seq // groups
    parts = seq // tokens
    reach = HALO + tokens
    row, part = mine // parts, mine % parts
    start = part * tokens
    rank_size = adapter_down_weight.shape[1]
    pairs = width // PAIR
    head_cols = query_key_value_weight.shape[2]

    places = jnp.arange(seq, dtype=jnp.int32)
    is_valid = (
        (places[None, :] < seq - 1)
        & (jnp.roll(example_numbers, -1, axis=1) == example_numbers)
        & (jnp.roll(completion, -1, axis=1) == 1)
    ).reshape(groups, tokens)
    before = (jnp.arange(tokens)[:, None] < jnp.arange(tokens)[None, :]).astype(jnp.bfloat16)
    rank = jnp.dot(is_valid.astype(jnp.bfloat16), before, preferred_element_type=jnp.float32).astype(jnp.int32)
    rank = jnp.where(is_valid, rank, -1)
    targets = jnp.roll(packed_token_rows, -1, axis=1).reshape(groups, tokens)
    need_rows = jnp.max(jnp.sum(is_valid.astype(jnp.float32), axis=1))

    need_slots, all_rounds = fetch_rows(embedding, packed_token_rows, parts, tokens, 1)
    agreed = agree(jnp.stack([need_slots, need_rows]), 2)
    rounds = ((agreed[0].astype(jnp.int32) + ROUND_ROWS - 1) // ROUND_ROWS).astype(jnp.int32)
    emb = all_rounds(rounds)

    wq = query_key_value_weight.reshape(width, 3 * head_cols)
    up_rows = adapter_up_weight.reshape(2 * rank_size, head_cols)
    if is_own_mesh():
        extra = jnp.pad(up_rows, ((0, 64 - 2 * rank_size), (0, 2 * head_cols)))
        wq = jnp.concatenate([wq, extra], axis=0)
        wq, wo, w1, w2 = gather_weights(
            [wq, attention_output_weight, feedforward_input_weight, feedforward_output_weight], 3
        )
        up_all = jnp.transpose(wq[:, width : width + 2 * rank_size, :head_cols], (1, 0, 2))
    else:
        wq, wo, w1, w2, up_all = gather_weights(
            [wq, attention_output_weight, feedforward_input_weight, feedforward_output_weight, up_rows], 3
        )
        wq = jnp.transpose(wq.reshape(groups, width, 3, head_cols), (1, 2, 0, 3)).reshape(width, 3, pairs, PAIR)
        wq = jnp.transpose(wq, (2, 0, 1, 3)).reshape(pairs, width, 3 * PAIR)
        up_all = jnp.transpose(up_all, (1, 0, 2))
    wo = wo.reshape(width, width)
    weights = (wq, wo, w1, w2)
    up_all = (ADAPTER_SCALE * up_all.reshape(2 * rank_size, width).astype(jnp.float32)).astype(jnp.bfloat16)
    up_query = jnp.pad(up_all[:rank_size], ((0, 128 - rank_size), (0, 0)))
    up_value = jnp.pad(up_all[rank_size:], ((rank_size, 128 - 2 * rank_size), (0, 0)))
    down = jnp.pad(adapter_down_weight.reshape(2 * rank_size, width), ((0, 128 - 2 * rank_size), (0, 0)))

    def window_of(values):
        first = lax.dynamic_slice_in_dim(values, jnp.maximum(start - HALO, 0), HALO, 0)
        return jnp.concatenate([first, lax.dynamic_slice_in_dim(values, start, tokens, 0)], axis=0)

    pos = window_of(positions)
    seg = window_of(lax.dynamic_index_in_dim(example_numbers, row, 0, keepdims=False))
    seg = jnp.where((jnp.arange(reach) < HALO) & (part == 0), -1, seg)
    my_rank = lax.dynamic_index_in_dim(rank, mine, 0, keepdims=False)
    my_valid = (my_rank >= 0).astype(jnp.float32)
    seg_col, seg_row = seg[:, None], seg[None, :]
    rows_c, pick, normed, low, query, key, value, one, two, fc = forward(
        emb, pos, seg_col, seg_row, my_rank[None, :], gains, down, up_query, up_value, weights
    )

    def head_of(count, collective):
        def run(rows_in):
            everyone = spread(rows_in[:count], collective).reshape(groups * count, width)
            spot = rank[:, None, :] == jnp.arange(count, dtype=jnp.int32)[None, :, None]
            wanted = jnp.sum(jnp.where(spot, targets[:, None, :], 0), axis=2) - mine * vocab_local
            grad, total = head(everyone, wanted.reshape(groups * count, 1), embedding)
            total = total[:, 0].reshape(groups, count)
            if is_own_mesh():
                lanes = -(-count // 128) * 128
                totals = swap(jnp.pad(total, ((0, 0), (0, lanes - count))), False, collective + 1)[:, :, :count]
            else:
                totals = lax.all_gather(total, "mp", axis=0)
            peak = jnp.max(totals, axis=0)
            lse = peak + jnp.log(jnp.sum(jnp.exp(totals - peak[None]), axis=0))
            grad = grad.reshape(groups, count, width) * jnp.exp(total - lse)[:, :, None]
            summed = collect(grad.astype(jnp.bfloat16), collective + 2)
            my_lse = lax.dynamic_index_in_dim(lse, mine, 0, keepdims=False)
            return (
                jnp.pad(summed, ((0, tokens - count), (0, 0))),
                jnp.pad(my_lse, (0, tokens - count)),
            )

        return run

    counts = (tokens * 9 // 16, tokens * 3 // 4, tokens)
    size = (agreed[1] > counts[0]).astype(jnp.int32) + (agreed[1] > counts[1]).astype(jnp.int32)
    grad_rows, lse = lax.switch(size, [head_of(count, 4 + 3 * i) for i, count in enumerate(counts)], rows_c)

    weight_col = (my_valid / global_token_count.astype(jnp.float32))[:, None]
    grads = backward(
        grad_rows, lse[None, :], my_rank[:, None], pick, weight_col, emb[reach:],
        (normed, low, query, key, value, one, two, fc), gains, seg_col, seg_row, up_query, up_value, weights,
    )

    dp_index = lax.axis_index("dp")
    cols = master.shape[2]
    flat = (4 * rank_size, cols)
    mask = jnp.broadcast_to((owners == dp_index).astype(jnp.float32).reshape(4 * rank_size, 1), flat)
    step = optimizer_step.astype(jnp.float32)
    scalars = jnp.stack([1.0 - jnp.power(BETA_ONE, step), 1.0 - jnp.power(BETA_TWO, step)])
    scalars = jnp.broadcast_to(jnp.pad(scalars, (0, 6))[:, None], (8, cols))
    loss, norm, new_first, new_second, new_master, new_copy = finish(
        grads, master.reshape(flat), first_moment.reshape(flat), second_moment.reshape(flat), mask, scalars, 13
    )
    shape = (1,) + master.shape
    return (
        loss,
        norm,
        new_first.reshape(shape),
        new_second.reshape(shape),
        new_master.reshape(shape),
        new_copy.reshape(shape),
    )


def solution(mesh):
    return jax.shard_map(
        local,
        mesh=mesh,
        in_specs=(
            P("dp", None),
            P("dp", None),
            P("dp", None),
            P(),
            P(),
            P(),
            P("mp", None),
            P(),
            P(),
            P(None, None, "mp"),
            P("mp", None),
            P(None, "mp"),
            P(None, "mp"),
            P(),
            P(None, None, "mp"),
            P(None, None, "mp"),
            P(None, None, "mp"),
            P(None, None, "mp"),
        ),
        out_specs=(
            P(),
            P(),
            P("dp", None, None, "mp"),
            P("dp", None, None, "mp"),
            P("dp", None, None, "mp"),
            P("dp", None, None, "mp"),
        ),
        check_vma=False,
    )
```

time: 3460 us -> 623 us (0.18)
  waiting for transfers between devices: 2270 us -> 0 us
  Pallas kernels: 0 us -> 505 us
  matrix products: 469 us -> 5.02 us
  blocking collectives: 408 us -> 0 us
  other arithmetic: 148 us -> 27.9 us
  local copies, waits for them, and re-layouts: 106 us -> 50.8 us
    reduce_scatter x20 -> x0, waiting for transfers between devices: 1210 us -> none  [the longest x4 352 us: local(): lax.psum_scatter(jnp.dot(rows_of(attn_mixed, jnp.int32(0), own_rows * lax...]
    all_gather x20 -> x0, waiting for transfers between devices: 691 us -> none  [the longest x4 174 us: local(): lax.all_gather(normed_two, 'mp', axis=0, tiled=True)]
    pallas_call x0 -> x10, Pallas kernels: none -> 505 us  [the longest x1 138 us: gather_weights(): pl.pallas_call(functools.partial(weight_kernel, sizes), out_shape=[jax.Sh...]
    dot_general x112 -> x2, matrix products: 469 us -> 5.02 us  [the longest x1 4.84 us: one_round(): jnp.dot(pick, got, preferred_element_type=jnp.float32).astype(jnp.bfloat16)]
    unnamed x50 -> x0, waiting for transfers between devices: 374 us -> none
    all_gather x12 -> x0, blocking collectives: 369 us -> none  [joined(): everything = jax.tree.map(lambda part: lax.all_gather(part, axis), shard)]
    reduce_sum x43 -> x5, other arithmetic: 95.7 us -> 7.21 us  [the longest x1 5.05 us: fetch_rows(): slot = jnp.sum(below.astype(jnp.int32), axis=2)]
    psum x1 -> x0, blocking collectives: 39.5 us -> none  [local(): lax.psum((jnp.sum(owned * owned), loss_part), ('dp', 'mp'))]
  transfers between devices with their start and end apart: 45 -> 0, of which waited for: 40 -> 0; matrix products, arithmetic and copies ran while one was open for 18% -> 0% of each run, Pallas kernels for 0% -> 0%
where the time goes in v1:
time: 623 us; the launch traced here: 615 us
  Pallas kernels  505 us (81%)
  local copies, waits for them, and re-layouts  50.8 us (8%)
  other arithmetic  27.9 us (4%)
  loops' own time  20.3 us (3%)
    pallas_call x1, Pallas kernels, gather_weights(): pl.pallas_call(functools.partial(weight_kernel, sizes), out_shape=[jax.Sh...  138 us
    pallas_call x1, Pallas kernels, head(): pl.pallas_call(functools.partial(head_kernel, tile, vocab // tile), out_s...  91.6 us
    pallas_call x1, Pallas kernels, spread(): pl.pallas_call(spread_kernel, out_shape=jax.ShapeDtypeStruct((LINE * SIDE...  60.6 us
    pallas_call x1, Pallas kernels, backward(): pl.pallas_call(backward_kernel, out_shape=jax.ShapeDtypeStruct((24, width...  56.9 us
    pallas_call x1, Pallas kernels, collect(): pl.pallas_call(collect_kernel, out_shape=jax.ShapeDtypeStruct(shape, part...  54.4 us
    pallas_call x1, Pallas kernels, forward(): pl.pallas_call(forward_kernel, out_shape=(jax.ShapeDtypeStruct((tokens, w...  40.9 us
    pallas_call x2, Pallas kernels, swap(): pl.pallas_call(functools.partial(swap_kernel, per_peer), out_shape=jax.Sh...  36.8 us
    another operation x1, loops' own time, local(): lax.switch(size, [head_of(count, 4 + 3 * i) for i, count in enumerate(cou...  20.1 us

profile of v1, /device:TPU:0, one launch (start us, length us, event | category | flops | bytes accessed | tf_op | source)
XLA Modules:
  0.0 614.6 jit_solution(13863266699277300883)
XLA Ops:
  2.2 0.8 dynamic-slice_bitcast_fusion
  2.9 0.8 dynamic_slice.41
  5.8 0.8 dynamic-slice_bitcast_fusion.1
  6.6 0.8 dynamic_slice.42
  10.9 0.8 slice.108
  11.7 0.8 slice.121
  12.6 0.8 slice.106
  13.4 0.8 and_and_fusion
  16.6 0.8 compare_select_fusion.weight_col
  17.4 1.0 constant_dynamic-slice_fusion.3
  18.6 0.8 fusion.8.seg_col
  19.8 2.6 gather_fusion.1
  22.7 4.3 and_reduce_fusion
  27.0 5.0 convert_reduce_fusion
  35.5 5.9 agree.1
  41.4 1.3 fusion.13
  44.7 1.4 copy.57
  46.5 1.0 fusion.6.refs_0_.refs_4_
  47.5 1.3 constant_dynamic-slice_fusion.2
  48.8 1.2 pad_maximum_fusion.pos
  50.0 10.9 %gather_fusion.2 = bf16[640,1024]{1,0:T(8,128)(2,1)} fusion(bf16[6400,1024]{1,0:T(8,128)(2,1)} %param.31, s32[1024]{0:T(1024)S(1)} %pad_clamp_fusion.2), kind=kCustom, calls=%fused_computation.2 | custom fusion | bytes 2624000 | tf_op jit(solution)/shard_map/jit(_take)/gather | solution.py:1107
  60.8 28.9 %swap_1.4 = bf16[8,80,1024]{2,1,0:T(8,128)(2,1)} custom-call(bf16[8,80,1024]{2,1,0:T(8,128)(2,1)} %bitcast.95), custom_call_target="tpu_custom_call" | custom-call | tf_op jit(solution)/shard_map/swap_1/pallas_call | solution.py:102
  89.8 4.8 convolution_convert_fusion.1
  94.9 2.3 slice.123.target_emb
  97.2 138.3 %gather_weights.1 = (bf16[8,1088,384]{2,1,0:T(8,128)(2,1)}, bf16[8,128,1024]{2,1,0:T(8,128)(2,1)}, bf16[8,1024,512]{2,1,0:T(8,128)(2,1)}, bf16[8,1024,512]{2,1,0:T(8,128)(2,1)}) custom-call(bf16[1088,384]{1,0:T(8,128)(2,1)} %fusion.6.refs_0_.refs_4_, bf16[128,1024]{1,0:T(8,128)(2,1)} %refs_5_.1, bf16[1024,512]{1,0:T(8,128)(2,1)} %refs_6_.1, ...), custom_call_target="tpu_custom_call" | custom-call | tf_op jit(solution)/shard_map/gather_weights/pallas_call | solution.py:320
  236.2 0.7 pad.48.up_value
  237.0 0.7 pad.47.up_query
  237.7 40.9 %forward.1 = (bf16[512,1024]{1,0:T(8,128)(2,1)S(1)}, f32[512,128]{1,0:T(8,128)}, bf16[640,1024]{1,0:T(8,128)(2,1)}, bf16[640,128]{1,0:T(8,128)(2,1)}, bf16[8,512...) custom-call(bf16[1152,1024]{1,0:T(8,128)(2,1)} %get-tuple-element.21, ...), custom_call_target="tpu_custom_call" | custom-call | tf_op jit(solution)/shard_map/forward/pallas_call | solution.py:773
  278.5 251.0 %conditional.1 = (bf16[512,1024]{1,0:T(8,128)(2,1)}, f32[1,512]{1,0:T(1,128)S(1)}) conditional(s32[]{:T(128)} %bitcast.15, (bf16[512,1024]{1,0:T(8,128)(2,1)S(1)}, s32[8,512]{1,0:T(8,128)S(1)}, s32[4,1024]{1,0:T(4,128)S(1)}, s32[]{:T(128)}, bf16[6400,1024]{1,0:T(8,128)(2,1)}) %tuple.68, (bf16[512,1024]{1,0:T(8,128)(2,1)S(1)}, ...), branch_computations={%region_9.13_spmd, %region_13.17_spmd, %region_17.21_spmd} | conditional | flops 14778372 | bytes 25825352 | solution.py:1237
  278.6 0.9 slice.80.own
  280.0 2.0 sub.171.target_ref
  282.1 60.6 %spread_4.1 = bf16[8,288,1024]{2,1,0:T(8,128)(2,1)} custom-call(bf16[288,1024]{1,0:T(8,128)(2,1)} %slice.80.own), custom_call_target="tpu_custom_call" | custom-call | tf_op jit(solution)/shard_map/cond/branch_0_fun/spread_4/pallas_call | solution.py:385
  342.7 91.6 %head_2304.1 = (f32[2304,1024]{1,0:T(8,128)}, f32[2304,128]{1,0:T(8,128)}) custom-call(bf16[2304,1024]{1,0:T(8,128)(2,1)} %bitcast.87, s32[2304,1]{1,0:T(8,128)} %sub.171.target_ref, bf16[6400,1024]{1,0:T(8,128)(2,1)} %get-tuple-element.165.table_ref), custom_call_target="tpu_custom_call" | custom-call | tf_op jit(solution)/shard_map/cond/branch_0_fun/head_2304/pallas_call | solution.py:537
  434.3 1.6 slice_reduce_fusion
  436.6 7.9 %swap_5.1 = f32[8,8,384]{2,1,0:T(8,128)} custom-call(f32[8,384]{1,0:T(8,128)} %pad.35.src), custom_call_target="tpu_custom_call" | custom-call | tf_op jit(solution)/shard_map/cond/branch_0_fun/swap_5/pallas_call | solution.py:102
  444.5 0.9 slice_reduce_fusion.1
  445.4 0.9 exponential_reduce_fusion
  446.4 6.5 %multiply_convert_fusion.src = bf16[8,288,1024]{2,1,0:T(8,128)(2,1)} fusion(f32[8,288,1024]{2,1,0:T(8,128)} %bitcast.90, f32[8,288]{1,0:T(8,128)S(1)} %get-tuple-element.252), kind=kLoop, calls=%fused_computation.12 | loop fusion | flops 4718592 | bytes 14164992 | tf_op jit(solution)/shard_map/cond/branch_0_fun/convert_element_type | solution.py:1226
  452.9 54.4 %collect_6.1 = bf16[288,1024]{1,0:T(8,128)(2,1)} custom-call(bf16[8,288,1024]{2,1,0:T(8,128)(2,1)} %multiply_convert_fusion.src), custom_call_target="tpu_custom_call" | custom-call | tf_op jit(solution)/shard_map/cond/branch_0_fun/collect_6/pallas_call | solution.py:467
  507.3 2.2 pad.36
  529.5 56.9 %backward.1 = f32[24,1024]{1,0:T(8,128)} custom-call(bf16[512,1024]{1,0:T(8,128)(2,1)} %get-tuple-element.216.grad_rows, f32[1,512]{1,0:T(1,128)S(1)} %get-tuple-element.217.lse_row, s32[512,1]{1,0:T(8,128)} %copy-done, f32[512,128]{1,0:T(8,128)} %get-tuple-element.218.pick, f32[512,1]{1,0:T(8,128)} %compare_select_fusion.weight_col, ...), custom_call_target="tpu_custom_call" | custom-call | tf_op jit(solution)/shard_map/backward/pallas_call | solution.py:943
  586.5 1.5 bitcast_bitcast_fusion.src
  588.0 19.8 %finish.1 = (f32[2,8,128]{2,1,0:T(8,128)}, f32[16,128]{1,0:T(8,128)}, f32[16,128]{1,0:T(8,128)}, f32[16,128]{1,0:T(8,128)}, bf16[16,128]{1,0:T(8,128)(2,1)}) custom-call(f32[8,24,128]{2,1,0:T(8,128)} %bitcast_bitcast_fusion.src, f32[16,128]{1,0:T(8,128)} %bitcast.105, f32[16,128]{1,0:T(8,128)} %bitcast.106, f32[16,128]{1,0:T(8,128)} %bitcast.107, ...), custom_call_target="tpu_custom_call" | custom-call | tf_op jit(solution)/shard_map/finish/pallas_call | solution.py:1047
  607.8 1.2 fusion.12
  609.0 1.3 copy.86
  610.3 1.3 copy.87
  611.6 1.3 copy.88
  612.9 1.3 copy.89
  (60 shorter events, 14.5 us)
Async XLA Ops:
  0.6 18.9 %copy-start.1 = (s32[4,1024]{1,0:T(4,128)S(1)}, s32[4,1024]{1,0:T(4,128)}, u32[]{:S(2)}) copy-start(s32[4,1024]{1,0:T(4,128)} %param.25) | copy-start | bytes 49156
  16.6 10.4 %copy-start = (s32[512,1]{1,0:T(8,128)}, s32[512,1]{1,0:T(8,128)S(1)}, u32[]{:S(2)}) copy-start(s32[512,1]{1,0:T(8,128)S(1)} %copy.60.rank_col) | copy-start | bytes 6148
  22.4 24.1 %copy-start.2 = (bf16[2,4,128]{2,1,0:T(4,128)(2,1)S(1)}, bf16[2,4,128]{2,1,0:T(4,128)(2,1)}, u32[]{:S(2)}) copy-start(bf16[2,4,128]{2,1,0:T(4,128)(2,1)} %param.39) | copy-start | bytes 6148
